TPU v7x, 32 devices: a whole 2x2x4 slice. The times are simulated.
32 devices in a mesh: enc: 8 (over z, x), dec: 2 (over y), grp: 2 (over core).
Axes of the slice: x: 2, y: 2, z: 4, core: 2. Of those that a mesh axis runs over, the one named last changes fastest.
Arguments:
- images: bfloat16 [32, 4, 32, 1280], P(('enc', 'dec', 'grp')), may hold values from -6 to 6
- ln_gain: float32 [1280], replicated, may hold values from 0.1 to 1.9
- ln_bias: float32 [1280], replicated, may hold values from -3 to 3
- fc1_weight: bfloat16 [5120, 1280], P('enc'), may hold values from -0.15625 to 0.15625
- fc1_bias: float32 [5120], P('enc'), may hold values from -3 to 3
- fc2_weight: bfloat16 [5120, 1280], P('enc'), may hold values from -0.078125 to 0.078125
- fc2_bias: float32 [1280], replicated, may hold values from -3 to 3
- key_weight: bfloat16 [1280, 512], replicated, may hold values from -0.15625 to 0.15625
- value_weight: bfloat16 [1280, 512], replicated, may hold values from -0.15625 to 0.15625
- text: bfloat16 [32, 128, 8192], P(('enc', 'grp')), may hold values from -6 to 6
- query_weight: bfloat16 [8192, 4096], P('enc', 'dec'), may hold values from -0.0625 to 0.0625
- tiles: int32 [8, 2, 2], replicated, may hold values from 1 to 4, as said below
- links: int32 [32, 2], P(('enc', 'grp')), may hold values from 0 to 1, as said below
- lengths: int32 [32], P(('enc', 'grp')), may hold values from 1 to 128
- state_grads: bfloat16 [32, 4, 32, 1280], P(('enc', 'dec', 'grp')), may hold values from -0.125 to 0.125
Outputs:
- context: bfloat16 [32, 128, 4096], P(('enc', 'grp'), None, 'dec')
- fc1_grad: float32 [5120, 1280], P(('enc', 'dec', 'grp'))
- fc2_grad: float32 [5120, 1280], P(('enc', 'dec', 'grp'))
Inputs may be any that keep to these rules, and one draw needn't show every extreme that they name: The 8 images that share their last two indices have 20 tiles together, and one of them has 4. `links`: every text is linked to at least one image.
All inputs are finite; a program needn't handle non-finite values.
Results may differ from a plain program's by a relative error of at most 0.017.
Values may be sent and summed in bfloat16 or wider, within the bound.
A program may use at most 128 MiB of HBM per device.

v0:
```python
import functools

import jax
import jax.numpy as jnp
from jax import lax
from jax.experimental import pallas as pl
from jax.experimental.pallas import tpu as pltpu
from jax.sharding import PartitionSpec as P


HEADS = 32
KV_HEADS = 4
HD = 128


EPSILON = 1e-06


def normalize_layer(values, gain, shift):
    middle = jnp.mean(values, axis=-1, keepdims=True)
    centered = values - middle
    spread = jnp.mean(centered * centered, axis=-1, keepdims=True)
    return centered * lax.rsqrt(spread + EPSILON) * gain + shift


def normalize_heads(values):
    return values * lax.rsqrt(jnp.mean(values * values, axis=-1, keepdims=True) + EPSILON)


def gelu_slope(values):
    return (
        0.5 * (1.0 + lax.erf(values * 0.7071067811865476))
        + values * jnp.exp(-0.5 * values * values) * 0.3989422804014327
    )


def encoder_rows(rows, fc1_weight, fc1_bias, fc2_weight):
    pre = (
        lax.dot_general(
            rows, fc1_weight, (((1,), (1,)), ((), ())), preferred_element_type=jnp.float32
        )
        + fc1_bias
    )
    hidden = jax.nn.gelu(pre, approximate=False).astype(jnp.bfloat16)
    partial_sum = jnp.dot(hidden, fc2_weight, preferred_element_type=jnp.float32)
    return (pre, hidden, partial_sum)


def weight_terms(rows, pre, hidden, cotangent, fc2_weight):
    hidden_grad = lax.dot_general(
        cotangent, fc2_weight, (((1,), (1,)), ((), ())), preferred_element_type=jnp.float32
    )
    second_term = lax.dot_general(
        hidden, cotangent, (((0,), (0,)), ((), ())), preferred_element_type=jnp.float32
    )
    pre_grad = (hidden_grad * gelu_slope(pre)).astype(jnp.bfloat16)
    first_term = lax.dot_general(
        pre_grad, rows, (((0,), (0,)), ((), ())), preferred_element_type=jnp.float32
    )
    return (first_term, second_term)


def project_heads(states, key_columns, value_columns, heads):
    width = states.shape[-1]
    key_raw = jnp.einsum(
        "rd,dhe->hre",
        states,
        key_columns.reshape(width, heads, HD),
        preferred_element_type=jnp.float32,
    )
    keys = normalize_heads(key_raw).astype(jnp.bfloat16)
    values = jnp.einsum(
        "rd,dhe->hre",
        states,
        value_columns.reshape(width, heads, HD),
        preferred_element_type=jnp.float32,
    ).astype(jnp.bfloat16)
    return (keys, values)


def shifted(values, axis, step):
    size = lax.axis_size(axis)
    return lax.ppermute(values, axis, [(i, (i + step) % size) for i in range(size)])


def swapped(values):
    return lax.ppermute(values, "enc", [(i, i ^ 1) for i in range(lax.axis_size("enc"))])


def share_text(text_rows):
    enc_count = lax.axis_size("enc")
    _, depth = text_rows.shape
    side = lax.axis_index("enc") % 2
    block = depth // enc_count
    even = jnp.stack([text_rows[:, i * block : (i + 1) * block] for i in range(0, enc_count, 2)])
    odd = jnp.stack([text_rows[:, i * block : (i + 1) * block] for i in range(1, enc_count, 2)])
    own = jnp.where(side == 0, even, odd)
    away = jnp.where(side == 0, odd, even)
    arrived = swapped(away)
    pair = jnp.concatenate([arrived, own], axis=1)
    return jnp.concatenate(
        [pair] + [shifted(pair, "grp", step) for step in range(1, lax.axis_size("grp"))], axis=1
    )


def project_queries(text_blocks, weight, before):
    grp_count = lax.axis_size("grp")
    ring = lax.axis_size("enc") // 2
    enc_count = lax.axis_size("enc")
    place = lax.axis_index("enc") // 2
    total = None
    for step in range(ring):
        if step == max(0, ring - 2):
            weight, _ = lax.optimization_barrier((weight, before))
        left = lax.dynamic_index_in_dim(text_blocks, (place - step) % ring, 0, keepdims=False)
        term = jnp.dot(left, weight, preferred_element_type=jnp.float32)
        total = term if total is None else total + term
        if step < ring - 1:
            weight = lax.ppermute(
                weight, "enc", [(i, (i + 2) % enc_count) for i in range(enc_count)]
            )
    columns = total.shape[1]
    total = total.reshape(grp_count, 2, -1, columns)
    arrived = swapped(total[:, 0].astype(jnp.bfloat16))
    raw = total[:, 1] + arrived.astype(jnp.float32)
    own = normalize_heads(raw.reshape(grp_count, -1, columns // HD, HD)).astype(jnp.bfloat16)
    blocks = jnp.stack(
        [own[0]] + [shifted(own[step], "grp", -step) for step in range(1, grp_count)], axis=1
    )
    start = (grp_count - lax.axis_index("grp")) % grp_count
    blocks = lax.dynamic_slice_in_dim(
        jnp.concatenate([blocks, blocks], axis=1), start, grp_count, 1
    )
    return blocks.reshape(blocks.shape[0], grp_count * columns)


def share_keys(states, key_weight, value_weight, first_head, kv_local):
    dec_count = lax.axis_size("dec")
    rows, _ = states.shape
    if dec_count == 2 and kv_local * dec_count == KV_HEADS:
        keys, values = project_heads(states, key_weight, value_weight, KV_HEADS)
        paired = jnp.stack([keys, values])
        own = lax.dynamic_slice_in_dim(paired, first_head, kv_local, 1)
        away = lax.dynamic_slice_in_dim(paired, KV_HEADS - kv_local - first_head, kv_local, 1)
        arrived = shifted(away, "dec", 1)
        first = lax.axis_index("dec") == 0
        paired = jnp.stack(
            [jnp.where(first, own, arrived), jnp.where(first, arrived, own)], axis=1
        )
        return (paired[0], paired[1])
    key_columns = lax.dynamic_slice_in_dim(key_weight, first_head * HD, kv_local * HD, 1)
    value_columns = lax.dynamic_slice_in_dim(value_weight, first_head * HD, kv_local * HD, 1)
    piece = lax.all_gather(states, "dec", axis=0, tiled=True)
    key_part, value_part = project_heads(piece, key_columns, value_columns, kv_local)
    shape = (kv_local, dec_count, rows, HD)
    return (
        key_part.reshape(shape).transpose(1, 0, 2, 3),
        value_part.reshape(shape).transpose(1, 0, 2, 3),
    )


def share_grads(terms):
    dec_count = lax.axis_size("dec")
    grp_count = lax.axis_size("grp")
    rows = terms.shape[1] // (dec_count * grp_count)
    if dec_count == 2 and grp_count == 2:
        parts = terms.reshape(2, dec_count, grp_count, rows, -1)
        grp_place = lax.axis_index("grp")
        dec_place = lax.axis_index("dec")
        kept = lax.dynamic_index_in_dim(parts, grp_place, 2, keepdims=False)
        away = lax.dynamic_index_in_dim(parts, 1 - grp_place, 2, keepdims=False)
        kept = kept + shifted(away.astype(jnp.bfloat16), "grp", 1).astype(jnp.float32)
        away = lax.dynamic_index_in_dim(kept, 1 - dec_place, 1, keepdims=False)
        kept = lax.dynamic_index_in_dim(kept, dec_place, 1, keepdims=False)
        kept = kept + shifted(away.astype(jnp.bfloat16), "dec", 1).astype(jnp.float32)
        return (kept[0], kept[1])
    summed = lax.psum_scatter(
        terms.astype(jnp.bfloat16), ("dec", "grp"), scatter_dimension=1, tiled=True
    ).astype(jnp.float32)
    return (summed[0], summed[1])


MESH = pl.DeviceIdType.MESH


def pick(table, place):
    return sum(jnp.where(place == i, value, 0) for i, value in enumerate(table))


def step_kernel(
    line,
    rows_ref,
    bias_ref,
    up_ref,
    down_ref,
    text_ref,
    weight_ref,
    query_ref,
    states_ref,
    up_grad_ref,
    down_grad_ref,
    tb,
    wb,
    fb,
    bb,
    bias_col,
    rows,
    pre,
    hid_t,
    hid,
    pg_t,
    po,
    psend,
    precv,
    msend,
    mrecv,
    gs1,
    gr1,
    gs2,
    gr2,
    gs3,
    gr3,
    local_sem,
    t_send,
    t_recv,
    y_send,
    y_recv,
    x_send,
    x_recv,
    s_send,
    s_recv,
    a_send,
    a_recv,
    p_send,
    p_recv,
    m_send,
    m_recv,
    g_send,
    g_recv,
):
    f32 = jnp.float32
    bf16 = jnp.bfloat16
    enc = lax.axis_index("enc")
    y = lax.axis_index("dec")
    g = lax.axis_index("grp")
    z, x = enc // 2, enc % 2
    other_x = ((z * 2 + 1 - x), y, g)
    other_y = (enc, 1 - y, g)
    other_g = (enc, y, 1 - g)

    def along(place):
        return (place * 2 + x, y, g)

    orders = [
        sorted([a for a in range(line) if a != p], key=lambda a: (-abs(a - p), min(a, line - 1 - a)))
        for p in range(line)
    ]
    order = [pick([orders[p][i] for p in range(line)], z) for i in range(line - 1)]
    text_rows, depth = tb.shape[2], tb.shape[3]
    half_cols = wb.shape[3]
    img = rows.shape[2]
    width = rows.shape[3]
    units = fb.shape[2]
    piece = units // 2
    part = units // 4

    barrier = pltpu.get_barrier_semaphore()
    for k in range(line):

        @pl.when(z != k)
        def _():
            pl.semaphore_signal(barrier, inc=1, device_id=along(k), device_id_type=MESH)

    for to in (other_x, other_y, other_g):
        pl.semaphore_signal(barrier, inc=1, device_id=to, device_id_type=MESH)
    pl.semaphore_wait(barrier, line + 2)

    def remote(src, dst, send, recv, to):
        return pltpu.make_async_remote_copy(
            src_ref=src, dst_ref=dst, send_sem=send, recv_sem=recv, device_id=to, device_id_type=MESH
        )

    def text_copy(i):
        b = order[i]
        at = pl.multiple_of((b * 2 + y) * depth, depth)
        return remote(
            text_ref.at[:, pl.ds(at, depth)], tb.at[z, y], t_send.at[i], t_recv.at[z], along(b)
        )

    def text_landed(a):
        return remote(tb.at[a, y], tb.at[a, y], t_send.at[0], t_recv.at[a], other_y)

    def text_relay(a):
        return remote(tb.at[a, y], tb.at[a, y], y_send.at[a], y_recv.at[a], other_y)

    def text_relayed(a):
        return remote(tb.at[a, 1 - y], tb.at[a, 1 - y], y_send.at[a], y_recv.at[a], other_y)

    weight_x = remote(
        weight_ref.at[:, pl.ds(pl.multiple_of(g * half_cols, half_cols), half_cols)],
        wb.at[x, g],
        x_send.at[0],
        x_recv.at[0],
        other_x,
    )
    weight_x_in = remote(wb.at[1 - x, g], wb.at[1 - x, g], x_send.at[0], x_recv.at[0], other_x)
    weight_s = remote(wb.at[1 - x, g], wb.at[1 - x, g], s_send.at[0], s_recv.at[0], other_g)
    weight_s_in = remote(wb.at[1 - x, 1 - g], wb.at[1 - x, 1 - g], s_send.at[0], s_recv.at[0], other_g)

    piece_at = pl.multiple_of(g * piece, piece)
    away_at = pl.multiple_of((1 - g) * piece, piece)

    def unit_x(ref, kind):
        return remote(
            ref.at[pl.ds(piece_at, piece)],
            fb.at[kind, x, pl.ds(piece_at, piece)],
            x_send.at[1],
            x_recv.at[1],
            other_x,
        )

    mine = fb.at[y, 1 - x, pl.ds(piece_at, piece)]
    unit_x_in = remote(mine, mine, x_send.at[1], x_recv.at[1], other_x)
    unit_s = remote(mine, mine, s_send.at[1], s_recv.at[1], other_g)
    unit_s_spot = fb.at[y, 1 - x, pl.ds(away_at, piece)]
    unit_s_in = remote(unit_s_spot, unit_s_spot, s_send.at[1], s_recv.at[1], other_g)
    unit_y = remote(mine, mine, y_send.at[line], y_recv.at[line], other_y)
    crossed = fb.at[1 - y, 1 - x, pl.ds(piece_at, piece)]
    unit_y_in = remote(crossed, crossed, y_send.at[line], y_recv.at[line], other_y)
    unit_s2 = remote(crossed, crossed, s_send.at[2], s_recv.at[2], other_g)
    unit_s2_spot = fb.at[1 - y, 1 - x, pl.ds(away_at, piece)]
    unit_s2_in = remote(unit_s2_spot, unit_s2_spot, s_send.at[2], s_recv.at[2], other_g)
    bias_x = remote(bias_ref, bb.at[x], x_send.at[2], x_recv.at[2], other_x)
    bias_x_in = remote(bb.at[1 - x], bb.at[1 - x], x_send.at[2], x_recv.at[2], other_x)

    def rows_copy(a, right, own):
        to = along(z + 1) if right else along(z - 1)
        src = rows_ref if own else rows.at[:, a]
        return remote(src, rows.at[:, a], a_send.at[1 if right else 0, a], a_recv.at[a], to)

    def rows_landed(a):
        return remote(rows.at[:, a], rows.at[:, a], a_send.at[0, a], a_recv.at[a], other_y)

    locals_ = [
        pltpu.make_async_copy(weight_ref.at[:, pl.ds(c * half_cols, half_cols)], wb.at[x, c], local_sem.at[c])
        for c in range(2)
    ] + [
        pltpu.make_async_copy(up_ref, fb.at[0, x], local_sem.at[2]),
        pltpu.make_async_copy(down_ref, fb.at[1, x], local_sem.at[3]),
        pltpu.make_async_copy(bias_ref, bb.at[x], local_sem.at[4]),
        pltpu.make_async_copy(rows_ref, rows.at[:, z], local_sem.at[5]),
    ] + [
        pltpu.make_async_copy(
            text_ref.at[:, pl.ds(pl.multiple_of((z * 2 + h) * depth, depth), depth)],
            tb.at[z, h],
            local_sem.at[6 + h],
        )
        for h in range(2)
    ]

    for i in range(line - 1):
        text_copy(i).start()
    weight_x.start()

    @pl.when(y == 0)
    def _():
        unit_x(up_ref, 0).start()

    @pl.when(y == 1)
    def _():
        unit_x(down_ref, 1).start()

    bias_x.start()

    @pl.when(z < line - 1)
    def _():
        rows_copy(z, True, True).start()

    @pl.when(z > 0)
    def _():
        rows_copy(z, False, True).start()

    for copy in locals_:
        copy.start()

    for i in reversed(range(line - 1)):
        text_landed(order[i]).wait_recv()
        text_relay(order[i]).start()
    weight_x_in.wait_recv()
    weight_s.start()
    for copy in locals_:
        copy.wait()

    def forward_rows(s):
        @pl.when(z - s >= 0)
        def _():
            rows_landed(z - s).wait_recv()

            @pl.when(z < line - 1)
            def _():
                rows_copy(z - s, True, False).start()

        @pl.when(z + s <= line - 1)
        def _():
            rows_landed(z + s).wait_recv()

            @pl.when(z > 0)
            def _():
                rows_copy(z + s, False, False).start()

    def has_incoming(a):
        return jnp.logical_or(
            jnp.logical_and(a > z, z > 0), jnp.logical_and(a < z, z < line - 1)
        )

    def next_slot(a):
        right = a > z
        to = jnp.where(right, z + 1, z - 1)
        slot = jnp.where(jnp.logical_and(to == a, jnp.logical_not(right)), line, a)
        return to, slot

    def sum_copy(a, c):
        to, slot = next_slot(a)
        return remote(psend.at[a, c], precv.at[slot, c], p_send.at[a, c], p_recv.at[slot, c], along(to))

    def sum_landed(slot, c):
        return remote(precv.at[slot, c], precv.at[slot, c], p_send.at[0, c], p_recv.at[slot, c], other_y)

    tile = 256

    def multiply(a, c, store):
        def body(t, _):
            cols = pl.ds(pl.multiple_of(t * tile, tile), tile)
            total = jnp.dot(tb[a, 0], wb[0, c, :, cols], preferred_element_type=f32)
            total = total + jnp.dot(tb[a, 1], wb[1, c, :, cols], preferred_element_type=f32)
            store(t, cols, total)
            return 0

        lax.fori_loop(0, half_cols // tile, body, 0)

    def product(i, c):
        a = order[i]

        def store(t, cols, total):
            psend[a, c, :, cols] = total.astype(bf16)

        multiply(a, c, store)

        @pl.when(jnp.logical_not(has_incoming(a)))
        def _():
            sum_copy(a, c).start()

    def add_incoming(i, c):
        a = order[i]

        @pl.when(has_incoming(a))
        def _():
            sum_landed(a, c).wait_recv()

            def body(t, _):
                r = pl.ds(pl.multiple_of(t * 16, 16), 16)
                psend[a, c, r] = (psend[a, c, r].astype(f32) + precv[a, c, r].astype(f32)).astype(bf16)
                return 0

            lax.fori_loop(0, text_rows // 16, body, 0)
            sum_copy(a, c).start()

    def products(i):
        text_relayed(order[i]).wait_recv()
        for c in range(2):
            product(i, c)

    weight_s_in.wait_recv()
    products(0)
    forward_rows(1)
    if line > 2:
        products(1)
    unit_x_in.wait_recv()
    unit_s.start()
    unit_y.start()
    for s in range(2, line):
        forward_rows(s)
    for i in range(2, line - 1):
        products(i)
    unit_y_in.wait_recv()
    unit_s2.start()
    for c in range(2):
        add_incoming(0, c)
    bias_x_in.wait_recv()
    unit_s_in.wait_recv()
    unit_s2_in.wait_recv()

    all_rows = line * img

    def up_body(q, _):
        k = q // 2
        at = pl.multiple_of((q % 2) * piece, piece)
        pre[k, pl.ds(at, piece)] = lax.dot_general(
            fb[0, k, pl.ds(at, piece)],
            rows[0].reshape(all_rows, width),
            (((1,), (1,)), ((), ())),
            preferred_element_type=f32,
        )
        return 0

    lax.fori_loop(0, 4, up_body, 0)
    for k in range(2):
        for t in range(units // 128):
            spot = slice(t * 128, (t + 1) * 128)
            bias_col[k, spot] = jnp.transpose(bb[k, :, spot])

    def gelu_body(r, _):
        k = r // (units // 16)
        at = pl.ds(pl.multiple_of((r % (units // 16)) * 16, 16), 16)
        value = pre[k, at] + bias_col[k, at, 0:1]
        phi = 0.5 * (1.0 + lax.erf(value * 0.7071067811865476))
        hid_t[k, at] = (value * phi).astype(bf16)
        pre[k, at] = phi + value * jnp.exp(-0.5 * value * value) * 0.3989422804014327
        return 0

    lax.fori_loop(0, 2 * units // 16, gelu_body, 0)

    def flip_body(t, _):
        for k in range(2):
            at = pl.ds(pl.multiple_of(t * 128, 128), 128)
            hid[k, :, at] = jnp.transpose(hid_t[k, at].astype(f32)).astype(bf16)
        return 0

    lax.fori_loop(0, units // 128, flip_body, 0)

    def down_body(t, _):
        cols = pl.ds(pl.multiple_of(t * tile, tile), tile)
        total = jnp.dot(hid[0], fb[1, 0, :, cols], preferred_element_type=f32)
        po[:, cols] = total + jnp.dot(hid[1], fb[1, 1, :, cols], preferred_element_type=f32)
        return 0

    lax.fori_loop(0, width // tile, down_body, 0)

    def state_copy(a):
        to, slot = next_slot(a)
        return remote(msend.at[a], mrecv.at[slot], m_send.at[a], m_recv.at[slot], along(to))

    def state_landed(slot):
        return remote(mrecv.at[slot], mrecv.at[slot], m_send.at[0], m_recv.at[slot], other_y)

    def send_state(i, first):
        a = order[i]
        waits = has_incoming(a)

        @pl.when(jnp.logical_not(waits) if first else waits)
        def _():
            if not first:
                state_landed(a).wait_recv()

            def body(t, _):
                r = pl.ds(pl.multiple_of(t * 16, 16), 16)
                value = po[pl.ds(pl.multiple_of(a * img + t * 16, 16), 16)]
                if not first:
                    value = value + mrecv[a, r].astype(f32)
                msend[a, r] = value.astype(bf16)
                return 0

            lax.fori_loop(0, img // 16, body, 0)
            state_copy(a).start()

    for i in range(line - 1):
        send_state(i, True)
    for i in range(1, line - 1):
        for c in range(2):
            add_incoming(i, c)
        send_state(i - 1, False)
    send_state(line - 2, False)

    def slope_body(q, _):
        k = q // 2
        at = pl.ds(pl.multiple_of((q % 2) * piece, piece), piece)
        grad = lax.dot_general(
            fb[1, k, at],
            rows[1].reshape(all_rows, width),
            (((1,), (1,)), ((), ())),
            preferred_element_type=f32,
        )
        pg_t[k, at] = (grad * pre[k, at]).astype(bf16)
        return 0

    lax.fori_loop(0, 4, slope_body, 0)

    def terms(kind, k, j, owner):
        at = pl.ds(pl.multiple_of(j * piece + owner * part, part), part)
        left = pg_t if kind == 0 else hid_t
        return jnp.dot(left[k, at], rows[kind].reshape(all_rows, width), preferred_element_type=f32)

    grads_s = remote(gs1, gr1, g_send.at[0], g_recv.at[0], other_g)
    grads_y = remote(gs2, gr2, g_send.at[1], g_recv.at[1], other_y)
    grads_x = remote(gs3, gr3, g_send.at[2], g_recv.at[2], other_x)
    for kind in range(2):

        def body(q, _, kind=kind):
            k, j = q // 2, q % 2
            gs1[kind, k, j] = terms(kind, k, j, 1 - g).astype(bf16)
            return 0

        lax.fori_loop(0, 4, body, 0)
    grads_s.start()
    grads_s.wait_recv()
    for kind in range(2):

        def body(k, _, kind=kind):
            gs2[kind, k] = (terms(kind, k, 1 - y, g) + gr1[kind, k, 1 - y].astype(f32)).astype(bf16)
            return 0

        lax.fori_loop(0, 2, body, 0)
    grads_y.start()

    for c in range(2):

        @pl.when(z > 0)
        def _():
            sum_landed(z, c).wait_recv()

        @pl.when(z < line - 1)
        def _():
            sum_landed(line, c).wait_recv()

        def store(t, cols, total, c=c):
            total = total + jnp.where(z > 0, precv[z, c, :, cols].astype(f32), 0.0)
            total = total + jnp.where(z < line - 1, precv[line, c, :, cols].astype(f32), 0.0)
            for h in range(tile // HD):
                head = total[:, h * HD : (h + 1) * HD]
                scale = lax.rsqrt(jnp.mean(head * head, axis=-1, keepdims=True) + EPSILON)
                at = pl.multiple_of(c * half_cols + t * tile + h * HD, HD)
                query_ref[:, pl.ds(at, HD)] = (head * scale).astype(bf16)

        multiply(z, c, store)

    states_ref[...] = po[pl.ds(pl.multiple_of(z * img, img), img)]

    @pl.when(z > 0)
    def _():
        state_landed(z).wait_recv()
        states_ref[...] += mrecv[z].astype(f32)

    @pl.when(z < line - 1)
    def _():
        state_landed(line).wait_recv()
        states_ref[...] += mrecv[line].astype(f32)

    grads_y.wait_recv()
    for kind in range(2):
        total = terms(kind, 1 - x, y, g) + gr1[kind, 1 - x, y].astype(f32)
        gs3[kind] = (total + gr2[kind, 1 - x].astype(f32)).astype(bf16)
    grads_x.start()
    grads_x.wait_recv()
    for kind, out in ((0, up_grad_ref), (1, down_grad_ref)):
        total = terms(kind, x, y, g) + gr1[kind, x, y].astype(f32)
        out[...] = total + gr2[kind, x].astype(f32) + gr3[kind].astype(f32)

    for i in range(line - 1):
        a = order[i]
        text_copy(i).wait_send()
        text_relay(a).wait_send()
        state_copy(a).wait_send()
        for c in range(2):
            sum_copy(a, c).wait_send()
    for copy in (weight_x, weight_s, unit_s, unit_y, unit_s2, bias_x, grads_s, grads_y, grads_x):
        copy.wait_send()
    unit_x(up_ref, 0).wait_send()

    for a in range(line):

        @pl.when(jnp.logical_and(a <= z, z < line - 1))
        def _():
            rows_copy(a, True, False).wait_send()

        @pl.when(jnp.logical_and(a >= z, z > 0))
        def _():
            rows_copy(a, False, False).wait_send()


def exchange(rows, bias, up, down, text, weight):
    line = lax.axis_size("enc") // 2
    text_rows = text.shape[0]
    depth, columns = weight.shape
    img, width = rows.shape[1:]
    units = up.shape[0]
    half = columns // 2
    f32, bf16 = jnp.float32, jnp.bfloat16
    dma = pltpu.SemaphoreType.DMA
    part = units // 4
    return pl.pallas_call(
        functools.partial(step_kernel, line),
        out_shape=[
            jax.ShapeDtypeStruct((text_rows, columns), bf16),
            jax.ShapeDtypeStruct((img, width), f32),
            jax.ShapeDtypeStruct((part, width), f32),
            jax.ShapeDtypeStruct((part, width), f32),
        ],
        in_specs=[pl.BlockSpec(memory_space=pl.ANY)] * 6,
        out_specs=[pl.BlockSpec(memory_space=pltpu.VMEM)] * 4,
        scratch_shapes=[
            pltpu.VMEM((line, 2, text_rows, depth), bf16),
            pltpu.VMEM((2, 2, depth, half), bf16),
            pltpu.VMEM((2, 2, units, width), bf16),
            pltpu.VMEM((2, 8, units), f32),
            pltpu.VMEM((2, units, 8), f32),
            pltpu.VMEM((2, line, img, width), bf16),
            pltpu.VMEM((2, units, line * img), f32),
            pltpu.VMEM((2, units, line * img), bf16),
            pltpu.VMEM((2, line * img, units), bf16),
            pltpu.VMEM((2, units, line * img), bf16),
            pltpu.VMEM((line * img, width), f32),
            pltpu.VMEM((line, 2, text_rows, half), bf16),
            pltpu.VMEM((line + 1, 2, text_rows, half), bf16),
            pltpu.VMEM((line, img, width), bf16),
            pltpu.VMEM((line + 1, img, width), bf16),
            pltpu.VMEM((2, 2, 2, part, width), bf16),
            pltpu.VMEM((2, 2, 2, part, width), bf16),
            pltpu.VMEM((2, 2, part, width), bf16),
            pltpu.VMEM((2, 2, part, width), bf16),
            pltpu.VMEM((2, part, width), bf16),
            pltpu.VMEM((2, part, width), bf16),
            dma((8,)),
            dma((line - 1,)),
            dma((line,)),
            dma((line + 1,)),
            dma((line + 1,)),
            dma((3,)),
            dma((3,)),
            dma((3,)),
            dma((3,)),
            dma((2, line)),
            dma((line,)),
            dma((line, 2)),
            dma((line + 1, 2)),
            dma((line,)),
            dma((line + 1,)),
            dma((3,)),
            dma((3,)),
        ],
        compiler_params=pltpu.CompilerParams(
            collective_id=0, has_side_effects=True, vmem_limit_bytes=67_000_000
        ),
        name="exchange",
    )(rows, bias, up, down, text, weight)


def attend(queries, keys, values, dec_tiles, links, lengths, slots, patch, length, dec_count):
    samples = links.shape[0]
    img_rows = slots * patch
    tile_index = jnp.arange(slots)
    kv_local, heads_each = queries.shape[2], queries.shape[3]
    live_keys = tile_index[None, :] < dec_tiles[:, None]
    live_keys = jnp.broadcast_to(live_keys[:, :, None], (dec_count, slots, patch)).reshape(
        dec_count, img_rows
    )
    allowed = (links[:, :, None] > 0) & live_keys[None, :, :]
    scores = jnp.einsum(
        "sqghd,jgkd->sghjkq", queries, keys, preferred_element_type=jnp.float32
    ) * HD ** (-0.5)
    weights = jnp.where(allowed[:, None, None, :, :, None], jnp.exp(scores), 0.0)
    totals = jnp.sum(weights, axis=(3, 4), keepdims=True)
    probs = (weights / totals).astype(jnp.bfloat16)
    mixed = jnp.einsum("sghjkq,jgkd->sqghd", probs, values, preferred_element_type=jnp.float32)
    valid = jnp.arange(length)[None, :] < lengths[:, None]
    return (
        jnp.where(valid[:, :, None, None, None], mixed, 0.0)
        .reshape(samples, length, kv_local * heads_each * HD)
        .astype(jnp.bfloat16)
    )


def on_column(
    images,
    ln_gain,
    ln_bias,
    fc1_weight,
    fc1_bias,
    fc2_weight,
    fc2_bias,
    key_weight,
    value_weight,
    text,
    query_weight,
    tiles,
    links,
    lengths,
    state_grads,
):
    dec_count = lax.axis_size("dec")
    enc_place = lax.axis_index("enc")
    dec_place = lax.axis_index("dec")
    grp_place = lax.axis_index("grp")
    slots, patch, width = images.shape[1:]
    img_rows = slots * patch
    samples, length = text.shape[:2]
    own_rows = images.reshape(img_rows, width)
    normed = normalize_layer(own_rows.astype(jnp.float32), ln_gain, ln_bias).astype(jnp.bfloat16)
    own_tiles = tiles[enc_place, dec_place, grp_place]
    own_live = jnp.arange(img_rows)[:, None] // patch < own_tiles
    cotangent = jnp.where(
        own_live, state_grads.reshape(img_rows, width), jnp.zeros((), state_grads.dtype)
    )
    bias = jnp.broadcast_to(fc1_bias[None, :], (8, fc1_bias.shape[0]))
    queries, summed, fc1_grad, fc2_grad = exchange(
        jnp.stack([normed, cotangent]),
        bias,
        fc1_weight,
        fc2_weight,
        text.reshape(samples * length, text.shape[2]),
        query_weight,
    )
    states = (own_rows.astype(jnp.float32) + summed + fc2_bias).astype(jnp.bfloat16)
    local_heads = query_weight.shape[1] // HD
    per_group = HEADS // KV_HEADS
    kv_local = max(1, local_heads // per_group)
    first_head = dec_place * local_heads // per_group
    keys, values = share_keys(states, key_weight, value_weight, first_head, kv_local)
    queries = queries.reshape(samples, length, kv_local, local_heads // kv_local, HD)
    context = attend(
        queries, keys, values, tiles[enc_place, :, grp_place], links, lengths, slots, patch, length, dec_count
    )
    return (context, fc1_grad, fc2_grad)


def on_device(
    images,
    ln_gain,
    ln_bias,
    fc1_weight,
    fc1_bias,
    fc2_weight,
    fc2_bias,
    key_weight,
    value_weight,
    text,
    query_weight,
    tiles,
    links,
    lengths,
    state_grads,
):
    dec_count = lax.axis_size("dec")
    grp_count = lax.axis_size("grp")
    enc_place = lax.axis_index("enc")
    dec_place = lax.axis_index("dec")
    grp_place = lax.axis_index("grp")
    slots = images.shape[1]
    patch = images.shape[2]
    width = images.shape[3]
    img_rows = slots * patch
    own_rows = images.reshape(img_rows, width)
    normed = normalize_layer(own_rows.astype(jnp.float32), ln_gain, ln_bias).astype(jnp.bfloat16)
    samples = text.shape[0]
    length = text.shape[1]
    text_rows = text.reshape(samples * length, text.shape[2])
    half = query_weight.shape[1] // grp_count
    own_half = lax.dynamic_slice_in_dim(query_weight, grp_place * half, half, 1)
    own_tiles = tiles[enc_place, dec_place, grp_place]
    tile_index = jnp.arange(slots)
    own_live = jnp.broadcast_to((tile_index < own_tiles)[:, None, None], (slots, patch, 1)).reshape(
        img_rows, 1
    )
    cotangent = jnp.where(
        own_live, state_grads.reshape(img_rows, width), jnp.zeros((), state_grads.dtype)
    )
    sent = jnp.stack([normed, cotangent])
    text_rows, own_half, _ = lax.optimization_barrier((text_rows, own_half, sent))
    both = lax.all_gather(sent, "enc", axis=1, tiled=True)
    gathered, all_cotangent = both[0], both[1]
    text_blocks = share_text(text_rows)
    pre, hidden, partial_full = encoder_rows(gathered, fc1_weight, fc1_bias, fc2_weight)
    partial_full = partial_full.astype(jnp.bfloat16)
    all_cotangent, _ = lax.optimization_barrier((all_cotangent, partial_full))
    first_term, second_term = weight_terms(gathered, pre, hidden, all_cotangent, fc2_weight)
    queries_of = project_queries(text_blocks, own_half, second_term)
    summed = lax.psum_scatter(
        partial_full, "enc", scatter_dimension=0, tiled=True
    ).astype(jnp.float32)
    states = (own_rows.astype(jnp.float32) + summed + fc2_bias).astype(jnp.bfloat16)
    local_heads = query_weight.shape[1] // HD
    per_group = HEADS // KV_HEADS
    kv_local = max(1, local_heads // per_group)
    first_head = dec_place * local_heads // per_group
    keys, values = share_keys(states, key_weight, value_weight, first_head, kv_local)
    heads_each = local_heads // kv_local
    queries = queries_of
    queries = queries.reshape(samples, length, kv_local, heads_each, HD)
    dec_tiles = tiles[enc_place, :, grp_place]
    live_keys = tile_index[None, :] < dec_tiles[:, None]
    live_keys = jnp.broadcast_to(live_keys[:, :, None], (dec_count, slots, patch)).reshape(
        dec_count, img_rows
    )
    allowed = (links[:, :, None] > 0) & live_keys[None, :, :]
    scores = jnp.einsum(
        "sqghd,jgkd->sghjkq", queries, keys, preferred_element_type=jnp.float32
    ) * HD ** (-0.5)
    weights = jnp.where(allowed[:, None, None, :, :, None], jnp.exp(scores), 0.0)
    totals = jnp.sum(weights, axis=(3, 4), keepdims=True)
    probs = (weights / totals).astype(jnp.bfloat16)
    mixed = jnp.einsum("sghjkq,jgkd->sqghd", probs, values, preferred_element_type=jnp.float32)
    valid = jnp.arange(length)[None, :] < lengths[:, None]
    context = (
        jnp.where(valid[:, :, None, None, None], mixed, 0.0)
        .reshape(samples, length, local_heads * HD)
        .astype(jnp.bfloat16)
    )
    fc1_grad, fc2_grad = share_grads(jnp.stack([first_term, second_term]))
    return (context, fc1_grad, fc2_grad)


def solution(mesh):
    in_specs = (
        P(("enc", "dec", "grp"), None, None, None),
        P(),
        P(),
        P("enc", None),
        P("enc"),
        P("enc", None),
        P(),
        P(),
        P(),
        P(("enc", "grp"), None, None),
        P("enc", "dec"),
        P(),
        P(("enc", "grp"), None),
        P(("enc", "grp")),
        P(("enc", "dec", "grp"), None, None, None),
    )
    out_specs = (
        P(("enc", "grp"), None, "dec"),
        P(("enc", "dec", "grp"), None),
        P(("enc", "dec", "grp"), None),
    )
    paired = mesh.shape["dec"] == 2 and mesh.shape["grp"] == 2 and mesh.shape["enc"] % 2 == 0
    if paired and mesh.shape["enc"] > 2:
        return jax.shard_map(
            on_column, mesh=mesh, in_specs=in_specs, out_specs=out_specs, check_vma=False
        )
    return jax.shard_map(
        on_device, mesh=mesh, in_specs=in_specs, out_specs=out_specs, check_vma=False
    )
```

profile of v0, /device:TPU:12, one launch (start us, length us, event | category | flops | bytes accessed | tf_op | source)
XLA Modules:
  0.0 241.6 jit_solution(10099146200338171632)
XLA Ops:
  0.6 1.1 convert_reduce_fusion
  1.8 1.2 multiply_reduce_fusion
  3.0 1.3 dynamic_slice.12
  4.3 0.7 fusion.36
  5.0 0.1 rsqrt.20
  5.1 1.1 bitcast_select_fusion.2
  6.1 1.3 fusion.23
  7.4 0.9 pad_maximum_fusion.rows_ref
  8.3 0.6 broadcast_in_dim.39.bias_ref
  8.9 217.7 %exchange.1 = (bf16[256,2048]{1,0:T(8,128)(2,1)}, f32[128,1280]{1,0:T(8,128)}, f32[160,1280]{1,0:T(8,128)}, f32[160,1280]{1,0:T(8,128)}) custom-call(bf16[2,128,1280]{2,1,0:T(8,128)(2,1)} %pad_maximum_fusion.rows_ref, f32[8,640]{1,0:T(8,128)} %broadcast_in_dim.39.bias_ref, bf16[640,1280]{1,0:T(8,128)(2,1)} %up_ref.1, bf16[640,1280]{1,0:T(8,128)(2,1)} %down_ref.1, ...), custom_call_target="tpu_custom_call" | custom-call | tf_op jit(solution)/shard_map/exchange/pallas_call | solution.py:690
  226.7 1.4 fusion.25
  228.0 2.0 multiply_reduce_fusion.1
  230.1 0.6 fusion.15
  230.8 1.3 collective-permute-start
  232.2 0.2 fusion.35
  232.4 0.2 copy.49
  232.8 0.1 and.45
  232.9 0.1 copy.29
  233.1 2.7 %collective-permute-done = bf16[2,2,128,128]{2,3,1,0:T(8,128)(2,1)S(1)} collective-permute-done((bf16[2,2,128,128]{2,3,1,0:T(8,128)(2,1)S(1)}, bf16[2,2,128,128]{2,3,1,0:T(8,128)(2,1)S(1)}, u32[]{:S(2)}, u32[]{:S(2)}) %collective-permute-start) | collective-permute-done | bytes 131104 | tf_op jit(solution)/shard_map/ppermute | solution.py:83
  235.9 1.2 fusion
  237.2 1.2 fusion.6
  238.5 1.3 copy.35
  239.8 0.9 copy.76
  240.7 0.9 copy.77
  (32 shorter events, 0.6 us)
Async XLA Ops:
  0.6 7.7 %copy-start.4 = (f32[640]{0:T(1024)S(1)}, f32[640]{0:T(1024)}, u32[]{:S(2)}) copy-start(f32[640]{0:T(1024)} %param.19) | copy-start | bytes 7684
  8.9 217.7 %copy-start.3 = (f32[1280]{0:T(1024)S(1)}, f32[1280]{0:T(1024)}, u32[]{:S(2)}) copy-start(f32[1280]{0:T(1024)} %param.21) | copy-start | bytes 15364
  226.6 3.5 %copy-start.6 = (bf16[1280,512]{1,0:T(8,128)(2,1)S(1)}, bf16[1280,512]{1,0:T(8,128)(2,1)}, u32[]{:S(2)}) copy-start(bf16[1280,512]{1,0:T(8,128)(2,1)} %param.23) | copy-start | bytes 3932164
  228.0 4.2 %copy-start.5 = (s32[8,2,2]{0,2,1:T(2,128)S(1)}, s32[8,2,2]{0,2,1:T(2,128)}, u32[]{:S(2)}) copy-start(s32[8,2,2]{0,2,1:T(2,128)} %param.26) | copy-start | bytes 388
  228.0 4.3 %copy-start = (bf16[256,2048]{1,0:T(8,128)(2,1)S(1)}, bf16[256,2048]{1,0:T(8,128)(2,1)}, u32[]{:S(2)}) copy-start(bf16[256,2048]{1,0:T(8,128)(2,1)} %get-tuple-element.8) | copy-start | bytes 3145732
  230.1 2.8 %copy-start.7 = (s32[2,2]{1,0:T(2,128)S(1)}, s32[2,2]{1,0:T(2,128)}, u32[]{:S(2)}) copy-start(s32[2,2]{1,0:T(2,128)} %param.27) | copy-start | bytes 52
  230.1 2.9 %copy-start.8 = (s32[2]{0:T(128)S(1)}, s32[2]{0:T(128)}, u32[]{:S(2)}) copy-start(s32[2]{0:T(128)} %param.28) | copy-start | bytes 28
  230.8 5.0 %collective-permute-start = (bf16[2,2,128,128]{2,3,1,0:T(8,128)(2,1)S(1)}, bf16[2,2,128,128]{2,3,1,0:T(8,128)(2,1)S(1)}, u32[]{:S(2)}, u32[]{:S(2)}) collective-permute-start(bf16[2,2,128,128]{2,3,1,0:T(8,128)(2,1)S(1)} %fusion.30), channel_id=1, source_target_pairs={{0,2},{2,0},{1,3},{3,1},{4,6},{6,4},{5,7},{7,5},{8,10},{10,8},{9,1... | collective-permute-start | bytes 393224 | tf_op jit(solution)/shard_map/ppermute | solution.py:83
  238.4 1.4 copy-start.2
  238.5 2.2 copy-start.1
where the time goes:
time: 246 us; the launch traced here: 242 us
  Pallas kernels  218 us (89%)
  other arithmetic  7.86 us (3%)
  local copies, waits for them, and re-layouts  5.95 us (2%)
  matrix products  5.14 us (2%)
  waiting for transfers between devices  2.73 us (1%)
    pallas_call x1, Pallas kernels, exchange(): pl.pallas_call(functools.partial(step_kernel, line), out_shape=[jax.Shape...  218 us
  transfers between devices with their start and end apart: 1, of which 1 were waited for; matrix products, arithmetic and copies ran while one was open for 0% of the time, Pallas kernels for 0%

commit v1 on v0

--- a/solution.py
+++ b/solution.py
@@ -251,11 +251,14 @@
     def along(place):
         return (place * 2 + x, y, g)
 
-    orders = [
-        sorted([a for a in range(line) if a != p], key=lambda a: (-abs(a - p), min(a, line - 1 - a)))
-        for p in range(line)
-    ]
+    orders, nearest = [], []
+    for p in range(line):
+        others = [a for a in range(line) if a != p]
+        others.sort(key=lambda a: (-abs(a - p), min(a, line - 1 - a)))
+        nearest.append(others[::-1])
+        orders.append(others[-1:] + others[:-1] if p in (0, line - 1) else others)
     order = [pick([orders[p][i] for p in range(line)], z) for i in range(line - 1)]
+    near = [pick([nearest[p][i] for p in range(line)], z) for i in range(line - 1)]
     text_rows, depth = tb.shape[2], tb.shape[3]
     half_cols = wb.shape[3]
     img = rows.shape[2]
@@ -281,7 +284,7 @@
         )
 
     def text_copy(i):
-        b = order[i]
+        b = near[i]
         at = pl.multiple_of((b * 2 + y) * depth, depth)
         return remote(
             text_ref.at[:, pl.ds(at, depth)], tb.at[z, y], t_send.at[i], t_recv.at[z], along(b)
@@ -362,6 +365,24 @@
         text_copy(i).start()
     weight_x.start()
 
+    @pl.when(z < line - 1)
+    def _():
+        rows_copy(z, True, True).start()
+
+    @pl.when(z > 0)
+    def _():
+        rows_copy(z, False, True).start()
+
+    for copy in locals_:
+        copy.start()
+
+    for i in range(line - 1):
+        text_landed(near[i]).wait_recv()
+        text_relay(near[i]).start()
+    weight_x_in.wait_recv()
+    weight_s.start()
+    weight_x.wait_send()
+
     @pl.when(y == 0)
     def _():
         unit_x(up_ref, 0).start()
@@ -371,23 +392,6 @@
         unit_x(down_ref, 1).start()
 
     bias_x.start()
-
-    @pl.when(z < line - 1)
-    def _():
-        rows_copy(z, True, True).start()
-
-    @pl.when(z > 0)
-    def _():
-        rows_copy(z, False, True).start()
-
-    for copy in locals_:
-        copy.start()
-
-    for i in reversed(range(line - 1)):
-        text_landed(order[i]).wait_recv()
-        text_relay(order[i]).start()
-    weight_x_in.wait_recv()
-    weight_s.start()
     for copy in locals_:
         copy.wait()
 
@@ -446,6 +450,9 @@
 
         multiply(a, c, store)
 
+    def send_product(i, c):
+        a = order[i]
+
         @pl.when(jnp.logical_not(has_incoming(a)))
         def _():
             sum_copy(a, c).start()
@@ -465,27 +472,27 @@
             lax.fori_loop(0, text_rows // 16, body, 0)
             sum_copy(a, c).start()
 
+    held = ((line - 2, 1),)
+
     def products(i):
         text_relayed(order[i]).wait_recv()
         for c in range(2):
             product(i, c)
+            if (i, c) not in held:
+                send_product(i, c)
 
     weight_s_in.wait_recv()
     products(0)
     forward_rows(1)
-    if line > 2:
-        products(1)
     unit_x_in.wait_recv()
     unit_s.start()
     unit_y.start()
+    for i in range(1, line - 1):
+        products(i)
     for s in range(2, line):
         forward_rows(s)
-    for i in range(2, line - 1):
-        products(i)
     unit_y_in.wait_recv()
     unit_s2.start()
-    for c in range(2):
-        add_incoming(0, c)
     bias_x_in.wait_recv()
     unit_s_in.wait_recv()
     unit_s2_in.wait_recv()
@@ -519,6 +526,7 @@
         return 0
 
     lax.fori_loop(0, 2 * units // 16, gelu_body, 0)
+    add_incoming(0, 0)
 
     def flip_body(t, _):
         for k in range(2):
@@ -563,13 +571,32 @@
             lax.fori_loop(0, img // 16, body, 0)
             state_copy(a).start()
 
-    for i in range(line - 1):
+    for i in range(1, line - 1):
         send_state(i, True)
-    for i in range(1, line - 1):
-        for c in range(2):
-            add_incoming(i, c)
-        send_state(i - 1, False)
-    send_state(line - 2, False)
+    send_product(line - 2, 1)
+    send_state(0, True)
+
+    def terms(kind, k, j, owner):
+        at = pl.ds(pl.multiple_of(j * piece + owner * part, part), part)
+        left = pg_t if kind == 0 else hid_t
+        return jnp.dot(left[k, at], rows[kind].reshape(all_rows, width), preferred_element_type=f32)
+
+    grads_s = [remote(gs1.at[m], gr1.at[m], g_send.at[m], g_recv.at[m], other_g) for m in range(2)]
+    grads_y = remote(gs2.at[0], gr2.at[0], g_send.at[2], g_recv.at[2], other_y)
+    grads_x = remote(gs2.at[1], gr2.at[1], g_send.at[3], g_recv.at[3], other_x)
+    grads_x2 = remote(gs3.at[0], gr3.at[0], g_send.at[4], g_recv.at[4], other_x)
+    grads_y2 = remote(gs3.at[1], gr3.at[1], g_send.at[5], g_recv.at[5], other_y)
+
+    def share_core(kind):
+        def body(q, _):
+            k, j = q // 2, q % 2
+            gs1[kind, k, j] = terms(kind, k, j, 1 - g).astype(bf16)
+            return 0
+
+        lax.fori_loop(0, 4, body, 0)
+        grads_s[kind].start()
+
+    share_core(1)
 
     def slope_body(q, _):
         k = q // 2
@@ -584,33 +611,40 @@
         return 0
 
     lax.fori_loop(0, 4, slope_body, 0)
-
-    def terms(kind, k, j, owner):
-        at = pl.ds(pl.multiple_of(j * piece + owner * part, part), part)
-        left = pg_t if kind == 0 else hid_t
-        return jnp.dot(left[k, at], rows[kind].reshape(all_rows, width), preferred_element_type=f32)
-
-    grads_s = remote(gs1, gr1, g_send.at[0], g_recv.at[0], other_g)
-    grads_y = remote(gs2, gr2, g_send.at[1], g_recv.at[1], other_y)
-    grads_x = remote(gs3, gr3, g_send.at[2], g_recv.at[2], other_x)
-    for kind in range(2):
-
-        def body(q, _, kind=kind):
-            k, j = q // 2, q % 2
-            gs1[kind, k, j] = terms(kind, k, j, 1 - g).astype(bf16)
-            return 0
-
-        lax.fori_loop(0, 4, body, 0)
-    grads_s.start()
-    grads_s.wait_recv()
-    for kind in range(2):
-
-        def body(k, _, kind=kind):
-            gs2[kind, k] = (terms(kind, k, 1 - y, g) + gr1[kind, k, 1 - y].astype(f32)).astype(bf16)
-            return 0
-
-        lax.fori_loop(0, 2, body, 0)
+    share_core(0)
+    add_incoming(0, 1)
+
+    grads_s[1].wait_recv()
+
+    def away_x(j, _):
+        gs2[1, j] = (terms(1, 1 - x, j, g) + gr1[1, 1 - x, j].astype(f32)).astype(bf16)
+        return 0
+
+    lax.fori_loop(0, 2, away_x, 0)
+    grads_x.start()
+    grads_s[0].wait_recv()
+
+    def away_y(k, _):
+        gs2[0, k] = (terms(0, k, 1 - y, g) + gr1[0, k, 1 - y].astype(f32)).astype(bf16)
+        return 0
+
+    lax.fori_loop(0, 2, away_y, 0)
     grads_y.start()
+    for i in range(1, line - 1):
+        add_incoming(i, 0)
+    for i in range(1, line - 2):
+        add_incoming(i, 1)
+    for i in range(line - 1):
+        send_state(i, False)
+    add_incoming(line - 2, 1)
+    grads_x.wait_recv()
+    total = terms(1, x, 1 - y, g) + gr1[1, x, 1 - y].astype(f32)
+    gs3[1] = (total + gr2[1, 1 - y].astype(f32)).astype(bf16)
+    grads_y2.start()
+    grads_y.wait_recv()
+    total = terms(0, 1 - x, y, g) + gr1[0, 1 - x, y].astype(f32)
+    gs3[0] = (total + gr2[0, 1 - x].astype(f32)).astype(bf16)
+    grads_x2.start()
 
     for c in range(2):
 
@@ -645,15 +679,11 @@
         state_landed(line).wait_recv()
         states_ref[...] += mrecv[line].astype(f32)
 
-    grads_y.wait_recv()
-    for kind in range(2):
-        total = terms(kind, 1 - x, y, g) + gr1[kind, 1 - x, y].astype(f32)
-        gs3[kind] = (total + gr2[kind, 1 - x].astype(f32)).astype(bf16)
-    grads_x.start()
-    grads_x.wait_recv()
-    for kind, out in ((0, up_grad_ref), (1, down_grad_ref)):
+    for kind, out in ((1, down_grad_ref), (0, up_grad_ref)):
+        (grads_x2, grads_y2)[kind].wait_recv()
         total = terms(kind, x, y, g) + gr1[kind, x, y].astype(f32)
-        out[...] = total + gr2[kind, x].astype(f32) + gr3[kind].astype(f32)
+        total = total + gr2[kind, (x, y)[kind]].astype(f32)
+        out[...] = total + gr3[kind].astype(f32)
 
     for i in range(line - 1):
         a = order[i]
@@ -662,7 +692,7 @@
         state_copy(a).wait_send()
         for c in range(2):
             sum_copy(a, c).wait_send()
-    for copy in (weight_x, weight_s, unit_s, unit_y, unit_s2, bias_x, grads_s, grads_y, grads_x):
+    for copy in (weight_s, unit_s, unit_y, unit_s2, bias_x, *grads_s, grads_y, grads_x, grads_x2, grads_y2):
         copy.wait_send()
     unit_x(up_ref, 0).wait_send()
 
@@ -734,8 +764,8 @@
             dma((line + 1, 2)),
             dma((line,)),
             dma((line + 1,)),
-            dma((3,)),
-            dma((3,)),
+            dma((6,)),
+            dma((6,)),
         ],
         compiler_params=pltpu.CompilerParams(
             collective_id=0, has_side_effects=True, vmem_limit_bytes=67_000_000
@@ -932,7 +962,7 @@
         P(("enc", "dec", "grp"), None),
     )
     paired = mesh.shape["dec"] == 2 and mesh.shape["grp"] == 2 and mesh.shape["enc"] % 2 == 0
-    if paired and mesh.shape["enc"] > 2:
+    if paired and mesh.shape["enc"] > 4:
         return jax.shard_map(
             on_column, mesh=mesh, in_specs=in_specs, out_specs=out_specs, check_vma=False
         )

time: 246 us -> 190 us (0.77); the launches traced: 242 us -> 189 us
  Pallas kernels: 218 us -> 163 us
    pallas_call x1, Pallas kernels: 218 us -> 163 us  [exchange(): pl.pallas_call(functools.partial(step_kernel, line), out_shape=[jax.Shape...]
where the time goes in v1:
time: 190 us; the launch traced here: 189 us
  Pallas kernels  163 us (86%)
  other arithmetic  7.86 us (4%)
  local copies, waits for them, and re-layouts  5.95 us (3%)
  matrix products  5.14 us (3%)
  waiting for transfers between devices  3.84 us (2%)
    pallas_call x1, Pallas kernels, exchange(): pl.pallas_call(functools.partial(step_kernel, line), out_shape=[jax.Shape...  163 us
    ppermute x1, waiting for transfers between devices, shifted(): lax.ppermute(values, axis, [(i, (i + step) % size) for i in range(size)])  3.84 us
  transfers between devices with their start and end apart: 1, of which 1 were waited for; matrix products, arithmetic and copies ran while one was open for 0% of the time, Pallas kernels for 0%

profile of v1, /device:TPU:12, one launch (start us, length us, event | category | flops | bytes accessed | tf_op | source)
XLA Modules:
  0.0 188.6 jit_solution(14174006073289168069)
XLA Ops:
  0.6 1.1 convert_reduce_fusion
  1.8 1.2 multiply_reduce_fusion
  3.0 1.3 dynamic_slice.12
  4.3 0.7 fusion.36
  5.0 0.1 rsqrt.20
  5.1 1.1 bitcast_select_fusion.2
  6.1 1.3 fusion.23
  7.4 0.9 pad_maximum_fusion.rows_ref
  8.3 0.6 broadcast_in_dim.39.bias_ref
  8.9 163.4 %exchange.1 = (bf16[256,2048]{1,0:T(8,128)(2,1)}, f32[128,1280]{1,0:T(8,128)}, f32[160,1280]{1,0:T(8,128)}, f32[160,1280]{1,0:T(8,128)}) custom-call(bf16[2,128,1280]{2,1,0:T(8,128)(2,1)} %pad_maximum_fusion.rows_ref, f32[8,640]{1,0:T(8,128)} %broadcast_in_dim.39.bias_ref, bf16[640,1280]{1,0:T(8,128)(2,1)} %up_ref.1, bf16[640,1280]{1,0:T(8,128)(2,1)} %down_ref.1, ...), custom_call_target="tpu_custom_call" | custom-call | tf_op jit(solution)/shard_map/exchange/pallas_call | solution.py:720
  172.3 1.4 fusion.25
  173.7 2.0 %multiply_reduce_fusion.1 = (f32[4,128]{1,0:T(4,128)S(1)}, f32[128,512]{0,1:S(1)}) fusion(bf16[128,1280]{1,0:T(8,128)(2,1)S(1)} %fusion.25, bf16[1280,512]{1,0:T(8,128)(2,1)} %param.22), kind=kOutput, calls=%fused_computation.35 | convolution fusion | flops 167902720 | bytes 1902592
  175.8 0.6 fusion.15
  176.5 1.6 collective-permute-start
  178.1 0.2 fusion.35
  178.3 0.2 copy.49
  178.7 0.1 and.45
  178.8 0.1 copy.29
  179.0 3.8 %collective-permute-done = bf16[2,2,128,128]{2,3,1,0:T(8,128)(2,1)S(1)} collective-permute-done((bf16[2,2,128,128]{2,3,1,0:T(8,128)(2,1)S(1)}, bf16[2,2,128,128]{2,3,1,0:T(8,128)(2,1)S(1)}, u32[]{:S(2)}, u32[]{:S(2)}) %collective-permute-start) | collective-permute-done | bytes 131104 | tf_op jit(solution)/shard_map/ppermute | solution.py:83
  182.9 1.2 fusion
  184.2 1.2 fusion.6
  185.5 1.3 copy.35
  186.8 0.9 copy.76
  187.7 0.9 copy.77
  (32 shorter events, 0.6 us)
Async XLA Ops:
  0.6 7.7 %copy-start.4 = (f32[640]{0:T(1024)S(1)}, f32[640]{0:T(1024)}, u32[]{:S(2)}) copy-start(f32[640]{0:T(1024)} %param.19) | copy-start | bytes 7684
  8.9 163.4 %copy-start.3 = (f32[1280]{0:T(1024)S(1)}, f32[1280]{0:T(1024)}, u32[]{:S(2)}) copy-start(f32[1280]{0:T(1024)} %param.21) | copy-start | bytes 15364
  172.3 3.5 %copy-start.6 = (bf16[1280,512]{1,0:T(8,128)(2,1)S(1)}, bf16[1280,512]{1,0:T(8,128)(2,1)}, u32[]{:S(2)}) copy-start(bf16[1280,512]{1,0:T(8,128)(2,1)} %param.23) | copy-start | bytes 3932164
  173.7 4.4 %copy-start.5 = (s32[8,2,2]{0,2,1:T(2,128)S(1)}, s32[8,2,2]{0,2,1:T(2,128)}, u32[]{:S(2)}) copy-start(s32[8,2,2]{0,2,1:T(2,128)} %param.26) | copy-start | bytes 388
  173.7 4.6 %copy-start = (bf16[256,2048]{1,0:T(8,128)(2,1)S(1)}, bf16[256,2048]{1,0:T(8,128)(2,1)}, u32[]{:S(2)}) copy-start(bf16[256,2048]{1,0:T(8,128)(2,1)} %get-tuple-element.8) | copy-start | bytes 3145732
  175.8 3.0 %copy-start.7 = (s32[2,2]{1,0:T(2,128)S(1)}, s32[2,2]{1,0:T(2,128)}, u32[]{:S(2)}) copy-start(s32[2,2]{1,0:T(2,128)} %param.27) | copy-start | bytes 52
  175.8 3.2 %copy-start.8 = (s32[2]{0:T(128)S(1)}, s32[2]{0:T(128)}, u32[]{:S(2)}) copy-start(s32[2]{0:T(128)} %param.28) | copy-start | bytes 28
  176.5 6.4 %collective-permute-start = (bf16[2,2,128,128]{2,3,1,0:T(8,128)(2,1)S(1)}, bf16[2,2,128,128]{2,3,1,0:T(8,128)(2,1)S(1)}, u32[]{:S(2)}, u32[]{:S(2)}) collective-permute-start(bf16[2,2,128,128]{2,3,1,0:T(8,128)(2,1)S(1)} %fusion.30), channel_id=1, source_target_pairs={{0,2},{2,0},{1,3},{3,1},{4,6},{6,4},{5,7},{7,5},{8,10},{10,8},{9,1... | collective-permute-start | bytes 393224 | tf_op jit(solution)/shard_map/ppermute | solution.py:83
  185.4 1.4 copy-start.2
  185.5 2.2 %copy-start.1 = (f32[160,1280]{1,0:T(8,128)S(1)}, f32[160,1280]{1,0:T(8,128)}, u32[]{:S(2)}) copy-start(f32[160,1280]{1,0:T(8,128)} %get-tuple-element.27) | copy-start | bytes 2457604

commit v2 on v1

--- a/solution.py
+++ b/solution.py
@@ -189,16 +189,30 @@
 
 def step_kernel(
     line,
-    rows_ref,
+    patch,
+    tiles_ref,
+    links_ref,
+    lengths_ref,
+    images_ref,
+    state_grads_ref,
+    gain_ref,
+    shift_ref,
     bias_ref,
     up_ref,
     down_ref,
+    down_bias_ref,
+    key_ref,
+    value_ref,
     text_ref,
     weight_ref,
-    query_ref,
-    states_ref,
+    context_ref,
     up_grad_ref,
     down_grad_ref,
+    own,
+    kw,
+    kv_send,
+    kv,
+    queries,
     tb,
     wb,
     fb,
@@ -237,6 +251,8 @@
     m_recv,
     g_send,
     g_recv,
+    k_send,
+    k_recv,
 ):
     f32 = jnp.float32
     bf16 = jnp.bfloat16
@@ -251,14 +267,12 @@
     def along(place):
         return (place * 2 + x, y, g)
 
-    orders, nearest = [], []
+    orders = []
     for p in range(line):
         others = [a for a in range(line) if a != p]
         others.sort(key=lambda a: (-abs(a - p), min(a, line - 1 - a)))
-        nearest.append(others[::-1])
-        orders.append(others[-1:] + others[:-1] if p in (0, line - 1) else others)
+        orders.append(others)
     order = [pick([orders[p][i] for p in range(line)], z) for i in range(line - 1)]
-    near = [pick([nearest[p][i] for p in range(line)], z) for i in range(line - 1)]
     text_rows, depth = tb.shape[2], tb.shape[3]
     half_cols = wb.shape[3]
     img = rows.shape[2]
@@ -284,7 +298,7 @@
         )
 
     def text_copy(i):
-        b = near[i]
+        b = order[i]
         at = pl.multiple_of((b * 2 + y) * depth, depth)
         return remote(
             text_ref.at[:, pl.ds(at, depth)], tb.at[z, y], t_send.at[i], t_recv.at[z], along(b)
@@ -310,39 +324,54 @@
     weight_s = remote(wb.at[1 - x, g], wb.at[1 - x, g], s_send.at[0], s_recv.at[0], other_g)
     weight_s_in = remote(wb.at[1 - x, 1 - g], wb.at[1 - x, 1 - g], s_send.at[0], s_recv.at[0], other_g)
 
-    piece_at = pl.multiple_of(g * piece, piece)
-    away_at = pl.multiple_of((1 - g) * piece, piece)
-
-    def unit_x(ref, kind):
+    def unit_rows(core, q):
+        return pl.ds(pl.multiple_of(core * piece + q * part, part), part)
+
+    def unit_x(ref, kind, q):
         return remote(
-            ref.at[pl.ds(piece_at, piece)],
-            fb.at[kind, x, pl.ds(piece_at, piece)],
-            x_send.at[1],
-            x_recv.at[1],
+            ref.at[unit_rows(g, q)],
+            fb.at[kind, x, unit_rows(g, q)],
+            x_send.at[1 + q],
+            x_recv.at[1 + q],
             other_x,
         )
 
-    mine = fb.at[y, 1 - x, pl.ds(piece_at, piece)]
-    unit_x_in = remote(mine, mine, x_send.at[1], x_recv.at[1], other_x)
-    unit_s = remote(mine, mine, s_send.at[1], s_recv.at[1], other_g)
-    unit_s_spot = fb.at[y, 1 - x, pl.ds(away_at, piece)]
-    unit_s_in = remote(unit_s_spot, unit_s_spot, s_send.at[1], s_recv.at[1], other_g)
-    unit_y = remote(mine, mine, y_send.at[line], y_recv.at[line], other_y)
-    crossed = fb.at[1 - y, 1 - x, pl.ds(piece_at, piece)]
-    unit_y_in = remote(crossed, crossed, y_send.at[line], y_recv.at[line], other_y)
-    unit_s2 = remote(crossed, crossed, s_send.at[2], s_recv.at[2], other_g)
-    unit_s2_spot = fb.at[1 - y, 1 - x, pl.ds(away_at, piece)]
-    unit_s2_in = remote(unit_s2_spot, unit_s2_spot, s_send.at[2], s_recv.at[2], other_g)
-    bias_x = remote(bias_ref, bb.at[x], x_send.at[2], x_recv.at[2], other_x)
-    bias_x_in = remote(bb.at[1 - x], bb.at[1 - x], x_send.at[2], x_recv.at[2], other_x)
-
-    def rows_copy(a, right, own):
+    def unit_copy(kind, core, q, send, recv, to):
+        spot = fb.at[kind, 1 - x, unit_rows(core, q)]
+        return remote(spot, spot, send, recv, to)
+
+    def unit_x_in(q):
+        return unit_copy(y, g, q, x_send.at[1 + q], x_recv.at[1 + q], other_x)
+
+    def unit_s(q):
+        return unit_copy(y, g, q, s_send.at[1 + q], s_recv.at[1 + q], other_g)
+
+    def unit_s_in(q):
+        return unit_copy(y, 1 - g, q, s_send.at[1 + q], s_recv.at[1 + q], other_g)
+
+    def unit_y(q):
+        return unit_copy(y, g, q, y_send.at[line + q], y_recv.at[line + q], other_y)
+
+    def unit_y_in(q):
+        return unit_copy(1 - y, g, q, y_send.at[line + q], y_recv.at[line + q], other_y)
+
+    def unit_s2(q):
+        return unit_copy(1 - y, g, q, s_send.at[3 + q], s_recv.at[3 + q], other_g)
+
+    def unit_s2_in(q):
+        return unit_copy(1 - y, 1 - g, q, s_send.at[3 + q], s_recv.at[3 + q], other_g)
+
+    bb[x] = bias_ref[...][None]
+    bias_x = remote(bb.at[x], bb.at[x], x_send.at[3], x_recv.at[3], other_x)
+    bias_x_in = remote(bb.at[1 - x], bb.at[1 - x], x_send.at[3], x_recv.at[3], other_x)
+
+    def rows_copy(m, a, right):
         to = along(z + 1) if right else along(z - 1)
-        src = rows_ref if own else rows.at[:, a]
-        return remote(src, rows.at[:, a], a_send.at[1 if right else 0, a], a_recv.at[a], to)
-
-    def rows_landed(a):
-        return remote(rows.at[:, a], rows.at[:, a], a_send.at[0, a], a_recv.at[a], other_y)
+        spot = rows.at[m, a]
+        return remote(spot, spot, a_send.at[1 if right else 0, m, a], a_recv.at[m, a], to)
+
+    def rows_landed(m, a):
+        return remote(rows.at[m, a], rows.at[m, a], a_send.at[0, m, a], a_recv.at[m, a], other_y)
 
     locals_ = [
         pltpu.make_async_copy(weight_ref.at[:, pl.ds(c * half_cols, half_cols)], wb.at[x, c], local_sem.at[c])
@@ -350,8 +379,8 @@
     ] + [
         pltpu.make_async_copy(up_ref, fb.at[0, x], local_sem.at[2]),
         pltpu.make_async_copy(down_ref, fb.at[1, x], local_sem.at[3]),
-        pltpu.make_async_copy(bias_ref, bb.at[x], local_sem.at[4]),
-        pltpu.make_async_copy(rows_ref, rows.at[:, z], local_sem.at[5]),
+        pltpu.make_async_copy(key_ref, kw.at[0], local_sem.at[5]),
+        pltpu.make_async_copy(value_ref, kw.at[1], local_sem.at[8]),
     ] + [
         pltpu.make_async_copy(
             text_ref.at[:, pl.ds(pl.multiple_of((z * 2 + h) * depth, depth), depth)],
@@ -364,53 +393,77 @@
     for i in range(line - 1):
         text_copy(i).start()
     weight_x.start()
-
-    @pl.when(z < line - 1)
-    def _():
-        rows_copy(z, True, True).start()
-
-    @pl.when(z > 0)
-    def _():
-        rows_copy(z, False, True).start()
-
-    for copy in locals_:
+    own_copies = [
+        pltpu.make_async_copy(images_ref, own.at[0], local_sem.at[9]),
+        pltpu.make_async_copy(state_grads_ref, own.at[1], local_sem.at[10]),
+    ]
+    for copy in own_copies + locals_:
         copy.start()
+    for copy in own_copies:
+        copy.wait()
+
+    def live_rows(j):
+        return tiles_ref[enc, j, g] * patch
+
+    own_live = live_rows(y)
+
+    def norm_body(t, _):
+        r = pl.ds(pl.multiple_of(t * 16, 16), 16)
+        normed = normalize_layer(own[0, r].astype(f32), gain_ref[...][None], shift_ref[...][None])
+        rows[0, z, r] = normed.astype(bf16)
+        row = t * 16 + lax.broadcasted_iota(jnp.int32, (16, width), 0)
+        rows[1, z, r] = jnp.where(row < own_live, own[1, r].astype(f32), 0.0).astype(bf16)
+        return 0
+
+    lax.fori_loop(0, img // 16, norm_body, 0)
+
+    for m in range(2):
+
+        @pl.when(z < line - 1)
+        def _(m=m):
+            rows_copy(m, z, True).start()
+
+        @pl.when(z > 0)
+        def _(m=m):
+            rows_copy(m, z, False).start()
 
     for i in range(line - 1):
-        text_landed(near[i]).wait_recv()
-        text_relay(near[i]).start()
+        text_landed(order[i]).wait_recv()
+        text_relay(order[i]).start()
     weight_x_in.wait_recv()
     weight_s.start()
     weight_x.wait_send()
 
     @pl.when(y == 0)
     def _():
-        unit_x(up_ref, 0).start()
+        for q in range(2):
+            unit_x(up_ref, 0, q).start()
 
     @pl.when(y == 1)
     def _():
-        unit_x(down_ref, 1).start()
+        for q in range(2):
+            unit_x(down_ref, 1, q).start()
 
     bias_x.start()
     for copy in locals_:
         copy.wait()
 
-    def forward_rows(s):
+    def forward_rows(m, s):
         @pl.when(z - s >= 0)
         def _():
-            rows_landed(z - s).wait_recv()
+            rows_landed(m, z - s).wait_recv()
 
             @pl.when(z < line - 1)
             def _():
-                rows_copy(z - s, True, False).start()
+                rows_copy(m, z - s, True).start()
 
         @pl.when(z + s <= line - 1)
         def _():
-            rows_landed(z + s).wait_recv()
+            rows_landed(m, z + s).wait_recv()
 
             @pl.when(z > 0)
             def _():
-                rows_copy(z + s, False, False).start()
+                rows_copy(m, z + s, False).start()
 
     def has_incoming(a):
         return jnp.logical_or(
@@ -472,7 +525,7 @@
             lax.fori_loop(0, text_rows // 16, body, 0)
             sum_copy(a, c).start()
 
-    held = ((line - 2, 1),)
+    held = ((line - 2, 0), (line - 2, 1))
 
     def products(i):
         text_relayed(order[i]).wait_recv()
@@ -481,21 +534,32 @@
             if (i, c) not in held:
                 send_product(i, c)
 
+    def relay_units(q):
+        unit_x_in(q).wait_recv()
+        unit_s(q).start()
+        unit_y(q).start()
+
     weight_s_in.wait_recv()
     products(0)
-    forward_rows(1)
-    unit_x_in.wait_recv()
-    unit_s.start()
-    unit_y.start()
-    for i in range(1, line - 1):
+    forward_rows(0, 1)
+    relay_units(0)
+    products(1)
+    add_incoming(0, 0)
+    for m in range(2):
+        forward_rows(m, 2 - m)
+    relay_units(1)
+    for i in range(2, line - 1):
         products(i)
-    for s in range(2, line):
-        forward_rows(s)
-    unit_y_in.wait_recv()
-    unit_s2.start()
+    unit_y_in(0).wait_recv()
+    unit_s2(0).start()
+    add_incoming(0, 1)
+    forward_rows(0, 3)
+    unit_y_in(1).wait_recv()
+    unit_s2(1).start()
     bias_x_in.wait_recv()
-    unit_s_in.wait_recv()
-    unit_s2_in.wait_recv()
+    for q in range(2):
+        unit_s_in(q).wait_recv()
+        unit_s2_in(q).wait_recv()
 
     all_rows = line * img
 
@@ -511,10 +575,11 @@
         return 0
 
     lax.fori_loop(0, 4, up_body, 0)
+    forward_rows(1, 2)
     for k in range(2):
         for t in range(units // 128):
             spot = slice(t * 128, (t + 1) * 128)
-            bias_col[k, spot] = jnp.transpose(bb[k, :, spot])
+            bias_col[k, spot] = jnp.transpose(jnp.broadcast_to(bb[k, :, spot], (8, 128)))
 
     def gelu_body(r, _):
         k = r // (units // 16)
@@ -525,8 +590,27 @@
         pre[k, at] = phi + value * jnp.exp(-0.5 * value * value) * 0.3989422804014327
         return 0
 
-    lax.fori_loop(0, 2 * units // 16, gelu_body, 0)
-    add_incoming(0, 0)
+    lax.fori_loop(0, 2 * units // 16, gelu_body, 0, unroll=4)
+
+    def terms(kind, k, j, owner):
+        at = pl.ds(pl.multiple_of(j * piece + owner * part, part), part)
+        left = pg_t if kind == 0 else hid_t
+        return jnp.dot(left[k, at], rows[kind].reshape(all_rows, width), preferred_element_type=f32)
+
+    grads_s = [remote(gs1.at[m], gr1.at[m], g_send.at[m], g_recv.at[m], other_g) for m in range(2)]
+    grads_y = remote(gs2.at[0], gr2.at[0], g_send.at[2], g_recv.at[2], other_y)
+    grads_x = remote(gs2.at[1], gr2.at[1], g_send.at[3], g_recv.at[3], other_x)
+    grads_x2 = remote(gs3.at[0], gr3.at[0], g_send.at[4], g_recv.at[4], other_x)
+    grads_y2 = remote(gs3.at[1], gr3.at[1], g_send.at[5], g_recv.at[5], other_y)
+
+    def share_core(kind):
+        def body(q, _):
+            k, j = q // 2, q % 2
+            gs1[kind, k, j] = terms(kind, k, j, 1 - g).astype(bf16)
+            return 0
+
+        lax.fori_loop(0, 4, body, 0)
+        grads_s[kind].start()
 
     def flip_body(t, _):
         for k in range(2):
@@ -571,31 +655,13 @@
             lax.fori_loop(0, img // 16, body, 0)
             state_copy(a).start()
 
-    for i in range(1, line - 1):
+    for i in range(line - 1):
         send_state(i, True)
-    send_product(line - 2, 1)
-    send_state(0, True)
-
-    def terms(kind, k, j, owner):
-        at = pl.ds(pl.multiple_of(j * piece + owner * part, part), part)
-        left = pg_t if kind == 0 else hid_t
-        return jnp.dot(left[k, at], rows[kind].reshape(all_rows, width), preferred_element_type=f32)
-
-    grads_s = [remote(gs1.at[m], gr1.at[m], g_send.at[m], g_recv.at[m], other_g) for m in range(2)]
-    grads_y = remote(gs2.at[0], gr2.at[0], g_send.at[2], g_recv.at[2], other_y)
-    grads_x = remote(gs2.at[1], gr2.at[1], g_send.at[3], g_recv.at[3], other_x)
-    grads_x2 = remote(gs3.at[0], gr3.at[0], g_send.at[4], g_recv.at[4], other_x)
-    grads_y2 = remote(gs3.at[1], gr3.at[1], g_send.at[5], g_recv.at[5], other_y)
-
-    def share_core(kind):
-        def body(q, _):
-            k, j = q // 2, q % 2
-            gs1[kind, k, j] = terms(kind, k, j, 1 - g).astype(bf16)
-            return 0
-
-        lax.fori_loop(0, 4, body, 0)
-        grads_s[kind].start()
-
+    for c in range(2):
+        send_product(line - 2, c)
+    add_incoming(1, 0)
+    add_incoming(2, 0)
+    forward_rows(1, 3)
     share_core(1)
 
     def slope_body(q, _):
@@ -612,7 +678,6 @@
 
     lax.fori_loop(0, 4, slope_body, 0)
     share_core(0)
-    add_incoming(0, 1)
 
     grads_s[1].wait_recv()
 
@@ -630,13 +695,11 @@
 
     lax.fori_loop(0, 2, away_y, 0)
     grads_y.start()
-    for i in range(1, line - 1):
-        add_incoming(i, 0)
-    for i in range(1, line - 2):
-        add_incoming(i, 1)
-    for i in range(line - 1):
-        send_state(i, False)
-    add_incoming(line - 2, 1)
+    add_incoming(1, 1)
+    send_state(0, False)
+    send_state(2, False)
+    add_incoming(2, 1)
+    send_state(1, False)
     grads_x.wait_recv()
     total = terms(1, x, 1 - y, g) + gr1[1, x, 1 - y].astype(f32)
     gs3[1] = (total + gr2[1, 1 - y].astype(f32)).astype(bf16)
@@ -646,7 +709,7 @@
     gs3[0] = (total + gr2[0, 1 - x].astype(f32)).astype(bf16)
     grads_x2.start()
 
-    for c in range(2):
+    def own_texts(c):
 
         @pl.when(z > 0)
         def _():
@@ -663,22 +726,76 @@
                 head = total[:, h * HD : (h + 1) * HD]
                 scale = lax.rsqrt(jnp.mean(head * head, axis=-1, keepdims=True) + EPSILON)
                 at = pl.multiple_of(c * half_cols + t * tile + h * HD, HD)
-                query_ref[:, pl.ds(at, HD)] = (head * scale).astype(bf16)
+                queries[:, pl.ds(at, HD)] = (head * scale).astype(bf16)
 
         multiply(z, c, store)
 
-    states_ref[...] = po[pl.ds(pl.multiple_of(z * img, img), img)]
+    slot_rows = pl.ds(pl.multiple_of(z * img, img), img)
+    po[slot_rows] = po[slot_rows] + own[0].astype(f32) + down_bias_ref[...][None]
 
     @pl.when(z > 0)
     def _():
         state_landed(z).wait_recv()
-        states_ref[...] += mrecv[z].astype(f32)
+        po[slot_rows] = po[slot_rows] + mrecv[z].astype(f32)
 
     @pl.when(z < line - 1)
     def _():
         state_landed(line).wait_recv()
-        states_ref[...] += mrecv[line].astype(f32)
-
+        po[slot_rows] = po[slot_rows] + mrecv[line].astype(f32)
+
+    states = po[slot_rows].astype(bf16)
+    local = kv.shape[2]
+    own_rows = pl.ds(pl.multiple_of(y * img, img), img)
+    away_rows = pl.ds(pl.multiple_of((1 - y) * img, img), img)
+    kv_copy = remote(kv_send, kv.at[:, own_rows], k_send, k_recv, other_y)
+    kv_in = remote(kv.at[:, away_rows], kv.at[:, away_rows], k_send, k_recv, other_y)
+    for sent in (True, False):
+        at = pl.multiple_of(((1 - y) if sent else y) * local, local)
+        spot = kv_send if sent else kv.at[:, own_rows]
+        raw = jnp.dot(states, kw[0, :, pl.ds(at, local)], preferred_element_type=f32)
+        for h in range(local // HD):
+            head = normalize_heads(raw[:, h * HD : (h + 1) * HD])
+            spot[0, :, h * HD : (h + 1) * HD] = head.astype(bf16)
+        raw = jnp.dot(states, kw[1, :, pl.ds(at, local)], preferred_element_type=f32)
+        spot[1] = raw.astype(bf16)
+        if sent:
+            kv_copy.start()
+
+    samples, length = context_ref.shape[:2]
+    group = half_cols // HD
+
+    def attend_texts(c):
+        head_cols = slice(c * HD, (c + 1) * HD)
+        key = lax.broadcasted_iota(jnp.int32, (length, 2 * img), 1)
+
+        def body(n, _):
+            r = pl.ds(pl.multiple_of(n * length, length), length)
+            limits = [jnp.where(links_ref[n, j] > 0, live_rows(j), 0) for j in range(2)]
+            allowed = key < jnp.where(key < img, limits[0], limits[1] + img)
+            valid = lax.broadcasted_iota(jnp.int32, (length, HD), 0) < lengths_ref[n]
+            for h in range(group):
+                cols = slice(c * half_cols + h * HD, c * half_cols + (h + 1) * HD)
+                score = lax.dot_general(
+                    queries[r, cols],
+                    kv[0, :, head_cols],
+                    (((1,), (1,)), ((), ())),
+                    preferred_element_type=f32,
+                )
+                weights = jnp.where(allowed, jnp.exp(score * HD ** (-0.5)), 0.0)
+                scale = 1.0 / jnp.sum(weights, axis=-1, keepdims=True)
+                mixed = jnp.dot(
+                    (weights * scale).astype(bf16), kv[1, :, head_cols], preferred_element_type=f32
+                )
+                context_ref[n, :, cols] = jnp.where(valid, mixed, 0.0).astype(bf16)
+            return 0
+
+        lax.fori_loop(0, samples, body, 0)
+
+    own_texts(0)
+    kv_in.wait_recv()
+    attend_texts(0)
+    own_texts(1)
+    attend_texts(1)
     for kind, out in ((1, down_grad_ref), (0, up_grad_ref)):
         (grads_x2, grads_y2)[kind].wait_recv()
         total = terms(kind, x, y, g) + gr1[kind, x, y].astype(f32)
@@ -692,46 +809,60 @@
         state_copy(a).wait_send()
         for c in range(2):
             sum_copy(a, c).wait_send()
-    for copy in (weight_s, unit_s, unit_y, unit_s2, bias_x, *grads_s, grads_y, grads_x, grads_x2, grads_y2):
+    for copy in (kv_copy, weight_s, bias_x, *grads_s, grads_y, grads_x, grads_x2, grads_y2):
         copy.wait_send()
-    unit_x(up_ref, 0).wait_send()
+    for q in range(2):
+        for copy in (unit_x(up_ref, 0, q), unit_s(q), unit_y(q), unit_s2(q)):
+            copy.wait_send()
 
     for a in range(line):
 
         @pl.when(jnp.logical_and(a <= z, z < line - 1))
         def _():
-            rows_copy(a, True, False).wait_send()
+            for m in range(2):
+                rows_copy(m, a, True).wait_send()
 
         @pl.when(jnp.logical_and(a >= z, z > 0))
         def _():
-            rows_copy(a, False, False).wait_send()
-
-
-def exchange(rows, bias, up, down, text, weight):
+            for m in range(2):
+                rows_copy(m, a, False).wait_send()
+
+
+def exchange(
+    tiles, links, lengths, images, state_grads, gain, shift, bias, up, down, down_bias, key, value, text, weight, patch
+):
     line = lax.axis_size("enc") // 2
-    text_rows = text.shape[0]
+    text_rows = text.shape[0] * text.shape[1]
     depth, columns = weight.shape
-    img, width = rows.shape[1:]
+    img, width = images.shape
     units = up.shape[0]
     half = columns // 2
+    local = key.shape[1] // 2
     f32, bf16 = jnp.float32, jnp.bfloat16
     dma = pltpu.SemaphoreType.DMA
     part = units // 4
+    smem = pl.BlockSpec(memory_space=pltpu.SMEM)
+    vmem = pl.BlockSpec(memory_space=pltpu.VMEM)
+    anywhere = pl.BlockSpec(memory_space=pl.ANY)
     return pl.pallas_call(
-        functools.partial(step_kernel, line),
+        functools.partial(step_kernel, line, patch),
         out_shape=[
-            jax.ShapeDtypeStruct((text_rows, columns), bf16),
-            jax.ShapeDtypeStruct((img, width), f32),
+            jax.ShapeDtypeStruct((*text.shape[:2], columns), bf16),
             jax.ShapeDtypeStruct((part, width), f32),
             jax.ShapeDtypeStruct((part, width), f32),
         ],
-        in_specs=[pl.BlockSpec(memory_space=pl.ANY)] * 6,
-        out_specs=[pl.BlockSpec(memory_space=pltpu.VMEM)] * 4,
+        in_specs=[smem] * 3 + [anywhere] * 2 + [vmem] * 3 + [anywhere] * 2 + [vmem] + [anywhere] * 4,
+        out_specs=[vmem] * 3,
         scratch_shapes=[
+            pltpu.VMEM((2, img, width), bf16),
+            pltpu.VMEM((2, width, 2 * local), bf16),
+            pltpu.VMEM((2, img, local), bf16),
+            pltpu.VMEM((2, 2 * img, local), bf16),
+            pltpu.VMEM((text_rows, columns), bf16),
             pltpu.VMEM((line, 2, text_rows, depth), bf16),
             pltpu.VMEM((2, 2, depth, half), bf16),
             pltpu.VMEM((2, 2, units, width), bf16),
-            pltpu.VMEM((2, 8, units), f32),
+            pltpu.VMEM((2, 1, units), f32),
             pltpu.VMEM((2, units, 8), f32),
             pltpu.VMEM((2, line, img, width), bf16),
             pltpu.VMEM((2, units, line * img), f32),
@@ -749,54 +880,31 @@
             pltpu.VMEM((2, 2, part, width), bf16),
             pltpu.VMEM((2, part, width), bf16),
             pltpu.VMEM((2, part, width), bf16),
-            dma((8,)),
+            dma((11,)),
             dma((line - 1,)),
             dma((line,)),
-            dma((line + 1,)),
-            dma((line + 1,)),
-            dma((3,)),
-            dma((3,)),
-            dma((3,)),
-            dma((3,)),
+            dma((line + 2,)),
+            dma((line + 2,)),
+            dma((4,)),
+            dma((4,)),
+            dma((5,)),
+            dma((5,)),
+            dma((2, 2, line)),
             dma((2, line)),
-            dma((line,)),
             dma((line, 2)),
             dma((line + 1, 2)),
             dma((line,)),
             dma((line + 1,)),
             dma((6,)),
             dma((6,)),
+            dma,
+            dma,
         ],
         compiler_params=pltpu.CompilerParams(
             collective_id=0, has_side_effects=True, vmem_limit_bytes=67_000_000
         ),
         name="exchange",
-    )(rows, bias, up, down, text, weight)
-
-
-def attend(queries, keys, values, dec_tiles, links, lengths, slots, patch, length, dec_count):
-    samples = links.shape[0]
-    img_rows = slots * patch
-    tile_index = jnp.arange(slots)
-    kv_local, heads_each = queries.shape[2], queries.shape[3]
-    live_keys = tile_index[None, :] < dec_tiles[:, None]
-    live_keys = jnp.broadcast_to(live_keys[:, :, None], (dec_count, slots, patch)).reshape(
-        dec_count, img_rows
-    )
-    allowed = (links[:, :, None] > 0) & live_keys[None, :, :]
-    scores = jnp.einsum(
-        "sqghd,jgkd->sghjkq", queries, keys, preferred_element_type=jnp.float32
-    ) * HD ** (-0.5)
-    weights = jnp.where(allowed[:, None, None, :, :, None], jnp.exp(scores), 0.0)
-    totals = jnp.sum(weights, axis=(3, 4), keepdims=True)
-    probs = (weights / totals).astype(jnp.bfloat16)
-    mixed = jnp.einsum("sghjkq,jgkd->sqghd", probs, values, preferred_element_type=jnp.float32)
-    valid = jnp.arange(length)[None, :] < lengths[:, None]
-    return (
-        jnp.where(valid[:, :, None, None, None], mixed, 0.0)
-        .reshape(samples, length, kv_local * heads_each * HD)
-        .astype(jnp.bfloat16)
-    )
+    )(tiles, links, lengths, images, state_grads, gain, shift, bias, up, down, down_bias, key, value, text.reshape(text_rows, -1), weight)
 
 
 def on_column(
@@ -816,38 +924,24 @@
     lengths,
     state_grads,
 ):
-    dec_count = lax.axis_size("dec")
-    enc_place = lax.axis_index("enc")
-    dec_place = lax.axis_index("dec")
-    grp_place = lax.axis_index("grp")
     slots, patch, width = images.shape[1:]
-    img_rows = slots * patch
-    samples, length = text.shape[:2]
-    own_rows = images.reshape(img_rows, width)
-    normed = normalize_layer(own_rows.astype(jnp.float32), ln_gain, ln_bias).astype(jnp.bfloat16)
-    own_tiles = tiles[enc_place, dec_place, grp_place]
-    own_live = jnp.arange(img_rows)[:, None] // patch < own_tiles
-    cotangent = jnp.where(
-        own_live, state_grads.reshape(img_rows, width), jnp.zeros((), state_grads.dtype)
-    )
-    bias = jnp.broadcast_to(fc1_bias[None, :], (8, fc1_bias.shape[0]))
-    queries, summed, fc1_grad, fc2_grad = exchange(
-        jnp.stack([normed, cotangent]),
-        bias,
+    context, fc1_grad, fc2_grad = exchange(
+        tiles,
+        links,
+        lengths,
+        images.reshape(slots * patch, width),
+        state_grads.reshape(slots * patch, width),
+        ln_gain,
+        ln_bias,
+        fc1_bias,
         fc1_weight,
         fc2_weight,
-        text.reshape(samples * length, text.shape[2]),
+        fc2_bias,
+        key_weight,
+        value_weight,
+        text,
         query_weight,
-    )
-    states = (own_rows.astype(jnp.float32) + summed + fc2_bias).astype(jnp.bfloat16)
-    local_heads = query_weight.shape[1] // HD
-    per_group = HEADS // KV_HEADS
-    kv_local = max(1, local_heads // per_group)
-    first_head = dec_place * local_heads // per_group
-    keys, values = share_keys(states, key_weight, value_weight, first_head, kv_local)
-    queries = queries.reshape(samples, length, kv_local, local_heads // kv_local, HD)
-    context = attend(
-        queries, keys, values, tiles[enc_place, :, grp_place], links, lengths, slots, patch, length, dec_count
+        patch,
     )
     return (context, fc1_grad, fc2_grad)
 
@@ -962,7 +1056,7 @@
         P(("enc", "dec", "grp"), None),
     )
     paired = mesh.shape["dec"] == 2 and mesh.shape["grp"] == 2 and mesh.shape["enc"] % 2 == 0
-    if paired and mesh.shape["enc"] > 4:
+    if paired and mesh.shape["enc"] == 8:
         return jax.shard_map(
             on_column, mesh=mesh, in_specs=in_specs, out_specs=out_specs, check_vma=False
         )

time: 190 us -> 161 us (0.85)
  Pallas kernels: 163 us -> 153 us
  other arithmetic: 7.86 us -> 0 us
  matrix products: 5.14 us -> 0 us
  waiting for transfers between devices: 3.84 us -> 0 us
    pallas_call x1, Pallas kernels: 163 us -> 153 us  [exchange(): pl.pallas_call(functools.partial(step_kernel, line, patch), out_shape=[ja...]
    ppermute x1 -> x0, waiting for transfers between devices: 3.84 us -> none  [shifted(): lax.ppermute(values, axis, [(i, (i + step) % size) for i in range(size)])]
    dot_general x3 -> x0, matrix products: 3.09 us -> none  [the longest x1 1.24 us: attend(): jnp.einsum('sqghd,jgkd->sghjkq', queries, keys, preferred_element_type=jn...]
    convert_element_type x2 -> x0, other arithmetic: 2.61 us -> none  [the longest x1 1.35 us: on_column(): (own_rows.astype(jnp.float32) + summed + fc2_bias).astype(jnp.bfloat16)]
    reduce_sum x2 -> x0, other arithmetic: 2.3 us -> none  [the longest x1 1.2 us: normalize_layer(): spread = jnp.mean(centered * centered, axis=-1, keepdims=True)]
    unnamed x22 -> x8, local copies, waits for them, and re-layouts: 3.37 us -> 5.57 us
    unnamed x1 -> x0, matrix products: 2.04 us -> none
  transfers between devices with their start and end apart: 1 -> 0, of which waited for: 1 -> 0; matrix products, arithmetic and copies ran while one was open for 0% -> 0% of each run, Pallas kernels for 0% -> 0%
where the time goes in v2:
time: 161 us; the launch traced here: 159 us
  Pallas kernels  153 us (95%)
  local copies, waits for them, and re-layouts  5.57 us (3%)
    pallas_call x1, Pallas kernels, exchange(): pl.pallas_call(functools.partial(step_kernel, line, patch), out_shape=[ja...  153 us
    unnamed x8, local copies, waits for them, and re-layouts  5.57 us

profile of v2, /device:TPU:12, one launch (start us, length us, event | category | flops | bytes accessed | tf_op | source)
XLA Modules:
  0.0 159.5 jit_solution(6138582375011647821)
XLA Ops:
  0.6 1.4 copy.18.tiles_ref
  2.0 153.3 %exchange.1 = (bf16[2,128,2048]{2,1,0:T(8,128)(2,1)}, f32[160,1280]{1,0:T(8,128)}, f32[160,1280]{1,0:T(8,128)}) custom-call(s32[8,2,2]{2,1,0:T(2,128)} %copy.18.tiles_ref, s32[2,2]{1,0:T(2,128)} %links_ref.1, s32[2]{0:T(128)} %lengths_ref.1, bf16[128,1280]{1,0:T(8,128)(2,1)} %bitcast.4, bf16[128,1280]{1,0:T(8,128)(2,1)} %bitcast.5, f32[1280]{0:T(1024)} %gain_ref.1, ...), custom_call_target="tpu_custom_call" | custom-call | tf_op jit(solution)/shard_map/exchange/pallas_call | solution.py:847
  155.2 0.0 copy-start.1
  155.3 0.0 copy-start
  155.3 2.4 %copy.22 = bf16[2,128,2048]{2,1,0:T(8,128)(2,1)} copy(bf16[2,128,2048]{2,1,0:T(8,128)(2,1)} %get-tuple-element.6) | data formatting | bytes 2097152
  157.7 0.0 copy-done.1
  157.7 0.9 copy.23
  158.6 0.0 copy-done
  158.6 0.9 copy.24
Async XLA Ops:
  155.2 2.4 %copy-start.1 = (f32[160,1280]{1,0:T(8,128)S(1)}, f32[160,1280]{1,0:T(8,128)}, u32[]{:S(2)}) copy-start(f32[160,1280]{1,0:T(8,128)} %get-tuple-element.7) | copy-start | bytes 2457604
  155.3 3.3 %copy-start = (f32[160,1280]{1,0:T(8,128)S(1)}, f32[160,1280]{1,0:T(8,128)}, u32[]{:S(2)}) copy-start(f32[160,1280]{1,0:T(8,128)} %get-tuple-element.8) | copy-start | bytes 2457604

commit v3 on v2

--- a/solution.py
+++ b/solution.py
@@ -213,6 +213,7 @@
     kv_send,
     kv,
     queries,
+    acc,
     tb,
     wb,
     fb,
@@ -313,16 +314,32 @@
     def text_relayed(a):
         return remote(tb.at[a, 1 - y], tb.at[a, 1 - y], y_send.at[a], y_recv.at[a], other_y)
 
-    weight_x = remote(
-        weight_ref.at[:, pl.ds(pl.multiple_of(g * half_cols, half_cols), half_cols)],
-        wb.at[x, g],
-        x_send.at[0],
-        x_recv.at[0],
-        other_x,
-    )
-    weight_x_in = remote(wb.at[1 - x, g], wb.at[1 - x, g], x_send.at[0], x_recv.at[0], other_x)
-    weight_s = remote(wb.at[1 - x, g], wb.at[1 - x, g], s_send.at[0], s_recv.at[0], other_g)
-    weight_s_in = remote(wb.at[1 - x, 1 - g], wb.at[1 - x, 1 - g], s_send.at[0], s_recv.at[0], other_g)
+    quarter = half_cols // 2
+
+    def weight_source(c, core):
+        at = pl.multiple_of(core * half_cols + c * quarter, quarter)
+        return weight_ref.at[:, pl.ds(at, quarter)]
+
+    def weight_spot(k, c, core):
+        return wb.at[k, c, :, pl.ds(pl.multiple_of(core * quarter, quarter), quarter)]
+
+    def weight_x(c):
+        return remote(
+            weight_source(c, g), weight_spot(x, c, g), x_send.at[4 + c], x_recv.at[4 + c], other_x
+        )
+
+    def weight_copy(c, core, send, recv, to):
+        spot = weight_spot(1 - x, c, core)
+        return remote(spot, spot, send, recv, to)
+
+    def weight_x_in(c):
+        return weight_copy(c, g, x_send.at[4 + c], x_recv.at[4 + c], other_x)
+
+    def weight_s(c):
+        return weight_copy(c, g, s_send.at[5 + c], s_recv.at[5 + c], other_g)
+
+    def weight_s_in(c):
+        return weight_copy(c, 1 - g, s_send.at[5 + c], s_recv.at[5 + c], other_g)
 
     def unit_rows(core, q):
         return pl.ds(pl.multiple_of(core * piece + q * part, part), part)
@@ -374,8 +391,9 @@
         return remote(rows.at[m, a], rows.at[m, a], a_send.at[0, m, a], a_recv.at[m, a], other_y)
 
     locals_ = [
-        pltpu.make_async_copy(weight_ref.at[:, pl.ds(c * half_cols, half_cols)], wb.at[x, c], local_sem.at[c])
+        pltpu.make_async_copy(weight_source(c, k), weight_spot(x, c, k), local_sem.at[11 + c * 2 + k])
         for c in range(2)
+        for k in range(2)
     ] + [
         pltpu.make_async_copy(up_ref, fb.at[0, x], local_sem.at[2]),
         pltpu.make_async_copy(down_ref, fb.at[1, x], local_sem.at[3]),
@@ -392,7 +410,8 @@
 
     for i in range(line - 1):
         text_copy(i).start()
-    weight_x.start()
+    for c in range(2):
+        weight_x(c).start()
     own_copies = [
         pltpu.make_async_copy(images_ref, own.at[0], local_sem.at[9]),
         pltpu.make_async_copy(state_grads_ref, own.at[1], local_sem.at[10]),
@@ -403,7 +422,7 @@
         copy.wait()
 
     def live_rows(j):
-        return tiles_ref[enc, j, g] * patch
+        return tiles_ref[j, g, enc] * patch
 
     own_live = live_rows(y)
 
@@ -427,27 +446,6 @@
         def _(m=m):
             rows_copy(m, z, False).start()
 
-    for i in range(line - 1):
-        text_landed(order[i]).wait_recv()
-        text_relay(order[i]).start()
-    weight_x_in.wait_recv()
-    weight_s.start()
-    weight_x.wait_send()
-
-    @pl.when(y == 0)
-    def _():
-        for q in range(2):
-            unit_x(up_ref, 0, q).start()
-
-    @pl.when(y == 1)
-    def _():
-        for q in range(2):
-            unit_x(down_ref, 1, q).start()
-
-    bias_x.start()
-    for copy in locals_:
-        copy.wait()
-
     def forward_rows(m, s):
         @pl.when(z - s >= 0)
         def _():
@@ -539,8 +537,41 @@
         unit_s(q).start()
         unit_y(q).start()
 
-    weight_s_in.wait_recv()
-    products(0)
+    def relay_text(i):
+        text_landed(order[i]).wait_recv()
+        text_relay(order[i]).start()
+
+    relay_text(0)
+    weight_x_in(0).wait_recv()
+    weight_s(0).start()
+    for copy in locals_:
+        copy.wait()
+    text_relayed(order[0]).wait_recv()
+    weight_s_in(0).wait_recv()
+    product(0, 0)
+    send_product(0, 0)
+    for i in range(1, line - 1):
+        relay_text(i)
+    weight_x_in(1).wait_recv()
+    weight_s(1).start()
+    for c in range(2):
+        weight_x(c).wait_send()
+
+    @pl.when(y == 0)
+    def _():
+        for q in range(2):
+            unit_x(up_ref, 0, q).start()
+
+    @pl.when(y == 1)
+    def _():
+        for q in range(2):
+            unit_x(down_ref, 1, q).start()
+
+    bias_x.start()
+
+    weight_s_in(1).wait_recv()
+    product(0, 1)
+    send_product(0, 1)
     forward_rows(0, 1)
     relay_units(0)
     products(1)
@@ -709,8 +740,13 @@
     gs3[0] = (total + gr2[0, 1 - x].astype(f32)).astype(bf16)
     grads_x2.start()
 
+    def own_products(c):
+        def store(t, cols, total):
+            acc[c, :, cols] = total
+
+        multiply(z, c, store)
+
     def own_texts(c):
-
         @pl.when(z > 0)
         def _():
             sum_landed(z, c).wait_recv()
@@ -719,16 +755,20 @@
         def _():
             sum_landed(line, c).wait_recv()
 
-        def store(t, cols, total, c=c):
-            total = total + jnp.where(z > 0, precv[z, c, :, cols].astype(f32), 0.0)
-            total = total + jnp.where(z < line - 1, precv[line, c, :, cols].astype(f32), 0.0)
-            for h in range(tile // HD):
-                head = total[:, h * HD : (h + 1) * HD]
-                scale = lax.rsqrt(jnp.mean(head * head, axis=-1, keepdims=True) + EPSILON)
-                at = pl.multiple_of(c * half_cols + t * tile + h * HD, HD)
-                queries[:, pl.ds(at, HD)] = (head * scale).astype(bf16)
-
-        multiply(z, c, store)
+        def body(t, _):
+            r = pl.ds(pl.multiple_of(t * 32, 32), 32)
+            for h in range(half_cols // HD):
+                spot = slice(h * HD, (h + 1) * HD)
+                head = acc[c, r, spot]
+                head = head + jnp.where(z > 0, precv[z, c, r, spot].astype(f32), 0.0)
+                head = head + jnp.where(z < line - 1, precv[line, c, r, spot].astype(f32), 0.0)
+                queries[r, spot] = normalize_heads(head).astype(bf16)
+            return 0
+
+        lax.fori_loop(0, text_rows // 32, body, 0)
+
+    for c in range(2):
+        own_products(c)
 
     slot_rows = pl.ds(pl.multiple_of(z * img, img), img)
     po[slot_rows] = po[slot_rows] + own[0].astype(f32) + down_bias_ref[...][None]
@@ -765,7 +805,6 @@
     group = half_cols // HD
 
     def attend_texts(c):
-        head_cols = slice(c * HD, (c + 1) * HD)
         key = lax.broadcasted_iota(jnp.int32, (length, 2 * img), 1)
 
         def body(n, _):
@@ -774,9 +813,12 @@
             allowed = key < jnp.where(key < img, limits[0], limits[1] + img)
             valid = lax.broadcasted_iota(jnp.int32, (length, HD), 0) < lengths_ref[n]
             for h in range(group):
-                cols = slice(c * half_cols + h * HD, c * half_cols + (h + 1) * HD)
+                shared = h // (group // 2)
+                head_cols = slice(shared * HD, (shared + 1) * HD)
+                first = shared * half_cols + c * quarter + (h % (group // 2)) * HD
+                cols = slice(first, first + HD)
                 score = lax.dot_general(
-                    queries[r, cols],
+                    queries[r, h * HD : (h + 1) * HD],
                     kv[0, :, head_cols],
                     (((1,), (1,)), ((), ())),
                     preferred_element_type=f32,
@@ -792,16 +834,16 @@
         lax.fori_loop(0, samples, body, 0)
 
     own_texts(0)
-    kv_in.wait_recv()
-    attend_texts(0)
-    own_texts(1)
-    attend_texts(1)
     for kind, out in ((1, down_grad_ref), (0, up_grad_ref)):
         (grads_x2, grads_y2)[kind].wait_recv()
         total = terms(kind, x, y, g) + gr1[kind, x, y].astype(f32)
         total = total + gr2[kind, (x, y)[kind]].astype(f32)
         out[...] = total + gr3[kind].astype(f32)
 
+    kv_in.wait_recv()
+    attend_texts(0)
+    own_texts(1)
+    attend_texts(1)
     for i in range(line - 1):
         a = order[i]
         text_copy(i).wait_send()
@@ -809,7 +851,7 @@
         state_copy(a).wait_send()
         for c in range(2):
             sum_copy(a, c).wait_send()
-    for copy in (kv_copy, weight_s, bias_x, *grads_s, grads_y, grads_x, grads_x2, grads_y2):
+    for copy in (kv_copy, weight_s(0), weight_s(1), bias_x, *grads_s, grads_y, grads_x, grads_x2, grads_y2):
         copy.wait_send()
     for q in range(2):
         for copy in (unit_x(up_ref, 0, q), unit_s(q), unit_y(q), unit_s2(q)):
@@ -858,7 +900,8 @@
             pltpu.VMEM((2, width, 2 * local), bf16),
             pltpu.VMEM((2, img, local), bf16),
             pltpu.VMEM((2, 2 * img, local), bf16),
-            pltpu.VMEM((text_rows, columns), bf16),
+            pltpu.VMEM((text_rows, half), bf16),
+            pltpu.VMEM((2, text_rows, half), f32),
             pltpu.VMEM((line, 2, text_rows, depth), bf16),
             pltpu.VMEM((2, 2, depth, half), bf16),
             pltpu.VMEM((2, 2, units, width), bf16),
@@ -880,15 +923,15 @@
             pltpu.VMEM((2, 2, part, width), bf16),
             pltpu.VMEM((2, part, width), bf16),
             pltpu.VMEM((2, part, width), bf16),
-            dma((11,)),
+            dma((15,)),
             dma((line - 1,)),
             dma((line,)),
             dma((line + 2,)),
             dma((line + 2,)),
-            dma((4,)),
-            dma((4,)),
-            dma((5,)),
-            dma((5,)),
+            dma((6,)),
+            dma((6,)),
+            dma((7,)),
+            dma((7,)),
             dma((2, 2, line)),
             dma((2, line)),
             dma((line, 2)),
@@ -926,7 +969,7 @@
 ):
     slots, patch, width = images.shape[1:]
     context, fc1_grad, fc2_grad = exchange(
-        tiles,
+        tiles.transpose(1, 2, 0),
         links,
         lengths,
         images.reshape(slots * patch, width),

time: 161 us -> 152 us (0.944); the launches traced: 159 us -> 152 us
  Pallas kernels: 153 us -> 147 us
    pallas_call x1, Pallas kernels: 153 us -> 147 us  [exchange(): pl.pallas_call(functools.partial(step_kernel, line, patch), out_shape=[ja...]
    unnamed x8 -> x7, local copies, waits for them, and re-layouts: 5.57 us -> 4.21 us
where the time goes in v3:
time: 152 us
  Pallas kernels  147 us (97%)
  local copies, waits for them, and re-layouts  4.21 us (3%)
    pallas_call x1, Pallas kernels, exchange(): pl.pallas_call(functools.partial(step_kernel, line, patch), out_shape=[ja...  147 us
    unnamed x7, local copies, waits for them, and re-layouts  4.21 us

profile of v3, /device:TPU:12, one launch (start us, length us, event | category | flops | bytes accessed | tf_op | source)
XLA Modules:
  0.0 152.2 jit_solution(1944044328358891557)
XLA Ops:
  0.6 147.4 %exchange.1 = (bf16[2,128,2048]{2,1,0:T(8,128)(2,1)}, f32[160,1280]{1,0:T(8,128)}, f32[160,1280]{1,0:T(8,128)}) custom-call(s32[2,2,8]{2,1,0:T(2,128)} %bitcast.7, s32[2,2]{1,0:T(2,128)} %links_ref.1, s32[2]{0:T(128)} %lengths_ref.1, bf16[128,1280]{1,0:T(8,128)(2,1)} %bitcast.5, bf16[128,1280]{1,0:T(8,128)(2,1)} %bitcast.6, f32[1280]{0:T(1024)} %gain_ref.1, ...), custom_call_target="tpu_custom_call" | custom-call | tf_op jit(solution)/shard_map/exchange/pallas_call | solution.py:889
  148.0 0.0 copy-start.1
  148.0 0.0 copy-start
  148.0 2.4 %copy.21 = bf16[2,128,2048]{2,1,0:T(8,128)(2,1)} copy(bf16[2,128,2048]{2,1,0:T(8,128)(2,1)} %get-tuple-element.6) | data formatting | bytes 2097152
  150.4 0.0 copy-done.1
  150.4 0.9 copy.22
  151.3 0.0 copy-done
  151.3 0.9 copy.23
Async XLA Ops:
  148.0 2.4 %copy-start.1 = (f32[160,1280]{1,0:T(8,128)S(1)}, f32[160,1280]{1,0:T(8,128)}, u32[]{:S(2)}) copy-start(f32[160,1280]{1,0:T(8,128)} %get-tuple-element.7) | copy-start | bytes 2457604
  148.0 3.3 %copy-start = (f32[160,1280]{1,0:T(8,128)S(1)}, f32[160,1280]{1,0:T(8,128)}, u32[]{:S(2)}) copy-start(f32[160,1280]{1,0:T(8,128)} %get-tuple-element.8) | copy-start | bytes 2457604

commit v4 on v3

--- a/solution.py
+++ b/solution.py
@@ -190,17 +190,17 @@
 def step_kernel(
     line,
     patch,
-    tiles_ref,
-    links_ref,
-    lengths_ref,
+    tiles_in,
+    links_in,
+    lengths_in,
     images_ref,
     state_grads_ref,
-    gain_ref,
-    shift_ref,
-    bias_ref,
+    gain_in,
+    shift_in,
+    bias_in,
     up_ref,
     down_ref,
-    down_bias_ref,
+    down_bias_in,
     key_ref,
     value_ref,
     text_ref,
@@ -208,6 +208,13 @@
     context_ref,
     up_grad_ref,
     down_grad_ref,
+    tiles_ref,
+    links_ref,
+    lengths_ref,
+    gain_ref,
+    shift_ref,
+    bias_ref,
+    down_bias_ref,
     own,
     kw,
     kv_send,
@@ -378,7 +385,6 @@
     def unit_s2_in(q):
         return unit_copy(1 - y, 1 - g, q, s_send.at[3 + q], s_recv.at[3 + q], other_g)
 
-    bb[x] = bias_ref[...][None]
     bias_x = remote(bb.at[x], bb.at[x], x_send.at[3], x_recv.at[3], other_x)
     bias_x_in = remote(bb.at[1 - x], bb.at[1 - x], x_send.at[3], x_recv.at[3], other_x)
 
@@ -412,7 +418,18 @@
         text_copy(i).start()
     for c in range(2):
         weight_x(c).start()
+    small = (
+        (tiles_in, tiles_ref),
+        (links_in, links_ref),
+        (lengths_in, lengths_ref),
+        (gain_in, gain_ref),
+        (shift_in, shift_ref),
+        (bias_in, bias_ref),
+        (down_bias_in, down_bias_ref),
+    )
     own_copies = [
+        pltpu.make_async_copy(src, dst, local_sem.at[15 + i]) for i, (src, dst) in enumerate(small)
+    ] + [
         pltpu.make_async_copy(images_ref, own.at[0], local_sem.at[9]),
         pltpu.make_async_copy(state_grads_ref, own.at[1], local_sem.at[10]),
     ]
@@ -420,6 +437,7 @@
         copy.start()
     for copy in own_copies:
         copy.wait()
+    bb[x] = bias_ref[...][None]
 
     def live_rows(j):
         return tiles_ref[j, g, enc] * patch
@@ -870,6 +888,30 @@
                 rows_copy(m, a, False).wait_send()
 
 
+def store_kernel(*refs):
+    count = len(refs) // 2
+    copies = [
+        pltpu.make_async_copy(refs[i], refs[count + i], refs[-1].at[i]) for i in range(count)
+    ]
+    for copy in copies:
+        copy.start()
+    for copy in copies:
+        copy.wait()
+
+
+def store_outputs(*values):
+    anywhere = pl.BlockSpec(memory_space=pl.ANY)
+    return pl.pallas_call(
+        store_kernel,
+        out_shape=[jax.ShapeDtypeStruct(value.shape, value.dtype) for value in values],
+        in_specs=[anywhere] * len(values),
+        out_specs=[anywhere] * len(values),
+        scratch_shapes=[pltpu.SemaphoreType.DMA((len(values),))],
+        compiler_params=pltpu.CompilerParams(vmem_limit_bytes=1 << 20),
+        name="store_outputs",
+    )(*values)
+
+
 def exchange(
     tiles, links, lengths, images, state_grads, gain, shift, bias, up, down, down_bias, key, value, text, weight, patch
 ):
@@ -883,19 +925,25 @@
     f32, bf16 = jnp.float32, jnp.bfloat16
     dma = pltpu.SemaphoreType.DMA
     part = units // 4
-    smem = pl.BlockSpec(memory_space=pltpu.SMEM)
     vmem = pl.BlockSpec(memory_space=pltpu.VMEM)
     anywhere = pl.BlockSpec(memory_space=pl.ANY)
     return pl.pallas_call(
         functools.partial(step_kernel, line, patch),
         out_shape=[
-            jax.ShapeDtypeStruct((*text.shape[:2], columns), bf16),
-            jax.ShapeDtypeStruct((part, width), f32),
-            jax.ShapeDtypeStruct((part, width), f32),
+            pltpu.VMEM((*text.shape[:2], columns), bf16),
+            pltpu.VMEM((part, width), f32),
+            pltpu.VMEM((part, width), f32),
         ],
-        in_specs=[smem] * 3 + [anywhere] * 2 + [vmem] * 3 + [anywhere] * 2 + [vmem] + [anywhere] * 4,
+        in_specs=[anywhere] * 15,
         out_specs=[vmem] * 3,
         scratch_shapes=[
+            pltpu.SMEM(tiles.shape, jnp.int32),
+            pltpu.SMEM(links.shape, jnp.int32),
+            pltpu.SMEM(lengths.shape, jnp.int32),
+            pltpu.VMEM(gain.shape, f32),
+            pltpu.VMEM(shift.shape, f32),
+            pltpu.VMEM(bias.shape, f32),
+            pltpu.VMEM(down_bias.shape, f32),
             pltpu.VMEM((2, img, width), bf16),
             pltpu.VMEM((2, width, 2 * local), bf16),
             pltpu.VMEM((2, img, local), bf16),
@@ -923,7 +971,7 @@
             pltpu.VMEM((2, 2, part, width), bf16),
             pltpu.VMEM((2, part, width), bf16),
             pltpu.VMEM((2, part, width), bf16),
-            dma((15,)),
+            dma((22,)),
             dma((line - 1,)),
             dma((line,)),
             dma((line + 2,)),
@@ -944,7 +992,7 @@
             dma,
         ],
         compiler_params=pltpu.CompilerParams(
-            collective_id=0, has_side_effects=True, vmem_limit_bytes=67_000_000
+            collective_id=0, has_side_effects=True, vmem_limit_bytes=64_200_000
         ),
         name="exchange",
     )(tiles, links, lengths, images, state_grads, gain, shift, bias, up, down, down_bias, key, value, text.reshape(text_rows, -1), weight)
@@ -986,7 +1034,7 @@
         query_weight,
         patch,
     )
-    return (context, fc1_grad, fc2_grad)
+    return tuple(store_outputs(context, fc1_grad, fc2_grad))
 
 
 def on_device(

time: 152 us -> 147 us (0.967)
  local copies, waits for them, and re-layouts: 4.21 us -> 0 us
    unnamed x7 -> x0, local copies, waits for them, and re-layouts: 4.21 us -> none
    pallas_call x1 -> x2, Pallas kernels: 147 us -> 147 us  [the longest x1 145 us: exchange(): pl.pallas_call(functools.partial(step_kernel, line, patch), out_shape=[pl...]
where the time goes in v4:
time: 147 us
  Pallas kernels  147 us (100%)
    pallas_call x1, Pallas kernels, exchange(): pl.pallas_call(functools.partial(step_kernel, line, patch), out_shape=[pl...  145 us

profile of v4, /device:TPU:12, one launch (start us, length us, event | category | flops | bytes accessed | tf_op | source)
XLA Modules:
  0.0 147.2 jit_solution(7212291953215479494)
XLA Ops:
  0.6 145.0 %exchange.1 = (bf16[2,128,2048]{2,1,0:T(8,128)(2,1)S(1)}, f32[160,1280]{1,0:T(8,128)S(1)}, f32[160,1280]{1,0:T(8,128)S(1)}) custom-call(s32[2,2,8]{2,1,0:T(2,128)} %bitcast.7, s32[2,2]{1,0:T(2,128)} %links_in.1, s32[2]{0:T(128)} %lengths_in.1, bf16[128,1280]{1,0:T(8,128)(2,1)} %bitcast.5, bf16[128,1280]{1,0:T(8,128)(2,1)} %bitcast.6, f32[1280]{0:T(1024)} %gain_in.1, ...), custom_call_target="tpu_custom_call" | custom-call | tf_op jit(solution)/shard_map/exchange/pallas_call | solution.py:930
  145.7 1.5 %store_outputs.1 = (bf16[2,128,2048]{2,1,0:T(8,128)(2,1)}, f32[160,1280]{1,0:T(8,128)}, f32[160,1280]{1,0:T(8,128)}) custom-call(bf16[2,128,2048]{2,1,0:T(8,128)(2,1)S(1)} %get-tuple-element.6.refs_0_, f32[160,1280]{1,0:T(8,128)S(1)} %get-tuple-element.7.refs_1_, f32[160,1280]{1,0:T(8,128)S(1)} %get-tuple-element.8.refs_2_), custom_call_target="tpu_custom_call" | custom-call | tf_op jit(solution)/shard_map/store_outputs/pallas_call | solution.py:904

commit v5 on v4

--- a/solution.py
+++ b/solution.py
@@ -492,12 +492,16 @@
         slot = jnp.where(jnp.logical_and(to == a, jnp.logical_not(right)), line, a)
         return to, slot
 
-    def sum_copy(a, c):
+    pieces = [slice(p * quarter, (p + 1) * quarter) for p in range(2)]
+
+    def sum_copy(a, c, p):
         to, slot = next_slot(a)
-        return remote(psend.at[a, c], precv.at[slot, c], p_send.at[a, c], p_recv.at[slot, c], along(to))
-
-    def sum_landed(slot, c):
-        return remote(precv.at[slot, c], precv.at[slot, c], p_send.at[0, c], p_recv.at[slot, c], other_y)
+        spot = precv.at[slot, c, :, pieces[p]]
+        return remote(psend.at[a, c, :, pieces[p]], spot, p_send.at[a, c, p], p_recv.at[slot, c, p], along(to))
+
+    def sum_landed(slot, c, p):
+        spot = precv.at[slot, c, :, pieces[p]]
+        return remote(spot, spot, p_send.at[0, c, p], p_recv.at[slot, c, p], other_y)
 
     tile = 256
 
@@ -524,22 +528,25 @@
 
         @pl.when(jnp.logical_not(has_incoming(a)))
         def _():
-            sum_copy(a, c).start()
+            for p in range(2):
+                sum_copy(a, c, p).start()
 
     def add_incoming(i, c):
         a = order[i]
 
         @pl.when(has_incoming(a))
         def _():
-            sum_landed(a, c).wait_recv()
-
-            def body(t, _):
-                r = pl.ds(pl.multiple_of(t * 16, 16), 16)
-                psend[a, c, r] = (psend[a, c, r].astype(f32) + precv[a, c, r].astype(f32)).astype(bf16)
-                return 0
-
-            lax.fori_loop(0, text_rows // 16, body, 0)
-            sum_copy(a, c).start()
+            for p in range(2):
+                sum_landed(a, c, p).wait_recv()
+
+                def body(t, _, cols=pieces[p]):
+                    r = pl.ds(pl.multiple_of(t * 32, 32), 32)
+                    total = psend[a, c, r, cols].astype(f32) + precv[a, c, r, cols].astype(f32)
+                    psend[a, c, r, cols] = total.astype(bf16)
+                    return 0
+
+                lax.fori_loop(0, text_rows // 32, body, 0)
+                sum_copy(a, c, p).start()
 
     held = ((line - 2, 0), (line - 2, 1))
 
@@ -764,26 +771,26 @@
 
         multiply(z, c, store)
 
-    def own_texts(c):
+    def own_texts(c, p):
         @pl.when(z > 0)
         def _():
-            sum_landed(z, c).wait_recv()
+            sum_landed(z, c, p).wait_recv()
 
         @pl.when(z < line - 1)
         def _():
-            sum_landed(line, c).wait_recv()
+            sum_landed(line, c, p).wait_recv()
 
         def body(t, _):
-            r = pl.ds(pl.multiple_of(t * 32, 32), 32)
-            for h in range(half_cols // HD):
-                spot = slice(h * HD, (h + 1) * HD)
+            r = pl.ds(pl.multiple_of(t * 64, 64), 64)
+            for h in range(quarter // HD):
+                spot = slice(p * quarter + h * HD, p * quarter + (h + 1) * HD)
                 head = acc[c, r, spot]
                 head = head + jnp.where(z > 0, precv[z, c, r, spot].astype(f32), 0.0)
                 head = head + jnp.where(z < line - 1, precv[line, c, r, spot].astype(f32), 0.0)
                 queries[r, spot] = normalize_heads(head).astype(bf16)
             return 0
 
-        lax.fori_loop(0, text_rows // 32, body, 0)
+        lax.fori_loop(0, text_rows // 64, body, 0, unroll=2)
 
     for c in range(2):
         own_products(c)
@@ -820,9 +827,9 @@
             kv_copy.start()
 
     samples, length = context_ref.shape[:2]
-    group = half_cols // HD
-
-    def attend_texts(c):
+    group = quarter // HD
+
+    def attend_texts(c, p):
         key = lax.broadcasted_iota(jnp.int32, (length, 2 * img), 1)
 
         def body(n, _):
@@ -830,13 +837,12 @@
             limits = [jnp.where(links_ref[n, j] > 0, live_rows(j), 0) for j in range(2)]
             allowed = key < jnp.where(key < img, limits[0], limits[1] + img)
             valid = lax.broadcasted_iota(jnp.int32, (length, HD), 0) < lengths_ref[n]
+            head_cols = slice(p * HD, (p + 1) * HD)
             for h in range(group):
-                shared = h // (group // 2)
-                head_cols = slice(shared * HD, (shared + 1) * HD)
-                first = shared * half_cols + c * quarter + (h % (group // 2)) * HD
+                first = p * half_cols + c * quarter + h * HD
                 cols = slice(first, first + HD)
                 score = lax.dot_general(
-                    queries[r, h * HD : (h + 1) * HD],
+                    queries[r, p * quarter + h * HD : p * quarter + (h + 1) * HD],
                     kv[0, :, head_cols],
                     (((1,), (1,)), ((), ())),
                     preferred_element_type=f32,
@@ -849,9 +855,10 @@
                 context_ref[n, :, cols] = jnp.where(valid, mixed, 0.0).astype(bf16)
             return 0
 
-        lax.fori_loop(0, samples, body, 0)
-
-    own_texts(0)
+        lax.fori_loop(0, samples, body, 0, unroll=True)
+
+    for p in range(2):
+        own_texts(0, p)
     for kind, out in ((1, down_grad_ref), (0, up_grad_ref)):
         (grads_x2, grads_y2)[kind].wait_recv()
         total = terms(kind, x, y, g) + gr1[kind, x, y].astype(f32)
@@ -859,16 +866,20 @@
         out[...] = total + gr3[kind].astype(f32)
 
     kv_in.wait_recv()
-    attend_texts(0)
-    own_texts(1)
-    attend_texts(1)
+    for p in range(2):
+        attend_texts(0, p)
+    for p in range(2):
+        own_texts(1, p)
+        attend_texts(1, p)
+
     for i in range(line - 1):
         a = order[i]
         text_copy(i).wait_send()
         text_relay(a).wait_send()
         state_copy(a).wait_send()
         for c in range(2):
-            sum_copy(a, c).wait_send()
+            for p in range(2):
+                sum_copy(a, c, p).wait_send()
     for copy in (kv_copy, weight_s(0), weight_s(1), bias_x, *grads_s, grads_y, grads_x, grads_x2, grads_y2):
         copy.wait_send()
     for q in range(2):
@@ -982,8 +993,8 @@
             dma((7,)),
             dma((2, 2, line)),
             dma((2, line)),
-            dma((line, 2)),
-            dma((line + 1, 2)),
+            dma((line, 2, 2)),
+            dma((line + 1, 2, 2)),
             dma((line,)),
             dma((line + 1,)),
             dma((6,)),

time: 147 us -> 146 us (level)
  Pallas kernels: 147 us -> 145 us
    pallas_call x1, Pallas kernels: 145 us -> 143 us  [exchange(): pl.pallas_call(functools.partial(step_kernel, line, patch), out_shape=[pl...]
where the time goes in v5:
time: 146 us
  Pallas kernels  145 us (99%)
    pallas_call x1, Pallas kernels, exchange(): pl.pallas_call(functools.partial(step_kernel, line, patch), out_shape=[pl...  143 us

profile of v5, /device:TPU:12, one launch (start us, length us, event | category | flops | bytes accessed | tf_op | source)
XLA Modules:
  0.0 145.6 jit_solution(10277558266771760904)
XLA Ops:
  0.6 143.4 %exchange.1 = (bf16[2,128,2048]{2,1,0:T(8,128)(2,1)S(1)}, f32[160,1280]{1,0:T(8,128)S(1)}, f32[160,1280]{1,0:T(8,128)S(1)}) custom-call(s32[2,2,8]{2,1,0:T(2,128)} %bitcast.7, s32[2,2]{1,0:T(2,128)} %links_in.1, s32[2]{0:T(128)} %lengths_in.1, bf16[128,1280]{1,0:T(8,128)(2,1)} %bitcast.5, bf16[128,1280]{1,0:T(8,128)(2,1)} %bitcast.6, f32[1280]{0:T(1024)} %gain_in.1, ...), custom_call_target="tpu_custom_call" | custom-call | tf_op jit(solution)/shard_map/exchange/pallas_call | solution.py:941
  144.1 1.5 %store_outputs.1 = (bf16[2,128,2048]{2,1,0:T(8,128)(2,1)}, f32[160,1280]{1,0:T(8,128)}, f32[160,1280]{1,0:T(8,128)}) custom-call(bf16[2,128,2048]{2,1,0:T(8,128)(2,1)S(1)} %get-tuple-element.6.refs_0_, f32[160,1280]{1,0:T(8,128)S(1)} %get-tuple-element.7.refs_1_, f32[160,1280]{1,0:T(8,128)S(1)} %get-tuple-element.8.refs_2_), custom_call_target="tpu_custom_call" | custom-call | tf_op jit(solution)/shard_map/store_outputs/pallas_call | solution.py:915

commit v6 on v5

--- a/solution.py
+++ b/solution.py
@@ -391,10 +391,10 @@
     def rows_copy(m, a, right):
         to = along(z + 1) if right else along(z - 1)
         spot = rows.at[m, a]
-        return remote(spot, spot, a_send.at[1 if right else 0, m, a], a_recv.at[m, a], to)
+        return remote(spot, spot, a_send.at[1 if right else 0], a_recv.at[m, a], to)
 
     def rows_landed(m, a):
-        return remote(rows.at[m, a], rows.at[m, a], a_send.at[0, m, a], a_recv.at[m, a], other_y)
+        return remote(rows.at[m, a], rows.at[m, a], a_send.at[0], a_recv.at[m, a], other_y)
 
     locals_ = [
         pltpu.make_async_copy(weight_source(c, k), weight_spot(x, c, k), local_sem.at[11 + c * 2 + k])
@@ -497,11 +497,11 @@
     def sum_copy(a, c, p):
         to, slot = next_slot(a)
         spot = precv.at[slot, c, :, pieces[p]]
-        return remote(psend.at[a, c, :, pieces[p]], spot, p_send.at[a, c, p], p_recv.at[slot, c, p], along(to))
+        return remote(psend.at[a, c, :, pieces[p]], spot, p_send, p_recv.at[slot, c, p], along(to))
 
     def sum_landed(slot, c, p):
         spot = precv.at[slot, c, :, pieces[p]]
-        return remote(spot, spot, p_send.at[0, c, p], p_recv.at[slot, c, p], other_y)
+        return remote(spot, spot, p_send, p_recv.at[slot, c, p], other_y)
 
     tile = 256
 
@@ -872,31 +872,31 @@
         own_texts(1, p)
         attend_texts(1, p)
 
+    sums = psend.at[pl.ds(0, line - 1)]
+    remote(sums, sums, p_send, p_recv.at[0, 0, 0], other_y).wait_send()
     for i in range(line - 1):
         a = order[i]
         text_copy(i).wait_send()
         text_relay(a).wait_send()
         state_copy(a).wait_send()
-        for c in range(2):
-            for p in range(2):
-                sum_copy(a, c, p).wait_send()
     for copy in (kv_copy, weight_s(0), weight_s(1), bias_x, *grads_s, grads_y, grads_x, grads_x2, grads_y2):
         copy.wait_send()
     for q in range(2):
         for copy in (unit_x(up_ref, 0, q), unit_s(q), unit_y(q), unit_s2(q)):
             copy.wait_send()
 
-    for a in range(line):
-
-        @pl.when(jnp.logical_and(a <= z, z < line - 1))
-        def _():
-            for m in range(2):
-                rows_copy(m, a, True).wait_send()
-
-        @pl.when(jnp.logical_and(a >= z, z > 0))
-        def _():
-            for m in range(2):
-                rows_copy(m, a, False).wait_send()
+    def rows_gone(way, first, count):
+        spot = rows.at[:, pl.ds(first, count)]
+        remote(spot, spot, a_send.at[way], a_recv.at[0, 0], other_y).wait_send()
+
+    for k in range(line):
+
+        @pl.when(z == k)
+        def _(k=k):
+            if k < line - 1:
+                rows_gone(1, 0, k + 1)
+            if k > 0:
+                rows_gone(0, k, line - k)
 
 
 def store_kernel(*refs):
@@ -991,9 +991,9 @@
             dma((6,)),
             dma((7,)),
             dma((7,)),
-            dma((2, 2, line)),
+            dma((2,)),
             dma((2, line)),
-            dma((line, 2, 2)),
+            dma,
             dma((line + 1, 2, 2)),
             dma((line,)),
             dma((line + 1,)),

time: 146 us -> 146 us (level)
  no operation moved by 1% of the time
where the time goes in v6:
time: 146 us; the launch traced here: 145 us
  Pallas kernels  145 us (99%)
    pallas_call x1, Pallas kernels, exchange(): pl.pallas_call(functools.partial(step_kernel, line, patch), out_shape=[pl...  143 us

profile of v6, /device:TPU:12, one launch (start us, length us, event | category | flops | bytes accessed | tf_op | source)
XLA Modules:
  0.0 145.3 jit_solution(7706635980328371460)
XLA Ops:
  0.6 143.2 %exchange.1 = (bf16[2,128,2048]{2,1,0:T(8,128)(2,1)S(1)}, f32[160,1280]{1,0:T(8,128)S(1)}, f32[160,1280]{1,0:T(8,128)S(1)}) custom-call(s32[2,2,8]{2,1,0:T(2,128)} %bitcast.7, s32[2,2]{1,0:T(2,128)} %links_in.1, s32[2]{0:T(128)} %lengths_in.1, bf16[128,1280]{1,0:T(8,128)(2,1)} %bitcast.5, bf16[128,1280]{1,0:T(8,128)(2,1)} %bitcast.6, f32[1280]{0:T(1024)} %gain_in.1, ...), custom_call_target="tpu_custom_call" | custom-call | tf_op jit(solution)/shard_map/exchange/pallas_call | solution.py:941
  143.8 1.5 %store_outputs.1 = (bf16[2,128,2048]{2,1,0:T(8,128)(2,1)}, f32[160,1280]{1,0:T(8,128)}, f32[160,1280]{1,0:T(8,128)}) custom-call(bf16[2,128,2048]{2,1,0:T(8,128)(2,1)S(1)} %get-tuple-element.6.refs_0_, f32[160,1280]{1,0:T(8,128)S(1)} %get-tuple-element.7.refs_1_, f32[160,1280]{1,0:T(8,128)S(1)} %get-tuple-element.8.refs_2_), custom_call_target="tpu_custom_call" | custom-call | tf_op jit(solution)/shard_map/store_outputs/pallas_call | solution.py:915

commit v7 on v6

--- a/solution.py
+++ b/solution.py
@@ -309,11 +309,11 @@
         b = order[i]
         at = pl.multiple_of((b * 2 + y) * depth, depth)
         return remote(
-            text_ref.at[:, pl.ds(at, depth)], tb.at[z, y], t_send.at[i], t_recv.at[z], along(b)
+            text_ref.at[:, pl.ds(at, depth)], tb.at[z, y], t_send, t_recv.at[z], along(b)
         )
 
     def text_landed(a):
-        return remote(tb.at[a, y], tb.at[a, y], t_send.at[0], t_recv.at[a], other_y)
+        return remote(tb.at[a, y], tb.at[a, y], t_send, t_recv.at[a], other_y)
 
     def text_relay(a):
         return remote(tb.at[a, y], tb.at[a, y], y_send.at[a], y_recv.at[a], other_y)
@@ -686,10 +686,10 @@
 
     def state_copy(a):
         to, slot = next_slot(a)
-        return remote(msend.at[a], mrecv.at[slot], m_send.at[a], m_recv.at[slot], along(to))
+        return remote(msend.at[a], mrecv.at[slot], m_send, m_recv.at[slot], along(to))
 
     def state_landed(slot):
-        return remote(mrecv.at[slot], mrecv.at[slot], m_send.at[0], m_recv.at[slot], other_y)
+        return remote(mrecv.at[slot], mrecv.at[slot], m_send, m_recv.at[slot], other_y)
 
     def send_state(i, first):
         a = order[i]
@@ -872,13 +872,15 @@
         own_texts(1, p)
         attend_texts(1, p)
 
+    texts = tb.at[pl.ds(0, line - 1), 0]
+    remote(texts, texts, t_send, t_recv.at[0], other_y).wait_send()
+    sums = msend.at[pl.ds(0, line - 1)]
+    remote(sums, sums, m_send, m_recv.at[0], other_y).wait_send()
     sums = psend.at[pl.ds(0, line - 1)]
     remote(sums, sums, p_send, p_recv.at[0, 0, 0], other_y).wait_send()
     for i in range(line - 1):
         a = order[i]
-        text_copy(i).wait_send()
         text_relay(a).wait_send()
-        state_copy(a).wait_send()
     for copy in (kv_copy, weight_s(0), weight_s(1), bias_x, *grads_s, grads_y, grads_x, grads_x2, grads_y2):
         copy.wait_send()
     for q in range(2):
@@ -983,7 +985,7 @@
             pltpu.VMEM((2, part, width), bf16),
             pltpu.VMEM((2, part, width), bf16),
             dma((22,)),
-            dma((line - 1,)),
+            dma,
             dma((line,)),
             dma((line + 2,)),
             dma((line + 2,)),
@@ -995,7 +997,7 @@
             dma((2, line)),
             dma,
             dma((line + 1, 2, 2)),
-            dma((line,)),
+            dma,
             dma((line + 1,)),
             dma((6,)),
             dma((6,)),

time: 146 us -> 145 us (level)
  no operation moved by 1% of the time
where the time goes in v7:
time: 145 us
  Pallas kernels  145 us (100%)
    pallas_call x1, Pallas kernels, exchange(): pl.pallas_call(functools.partial(step_kernel, line, patch), out_shape=[pl...  143 us

profile of v7, /device:TPU:12, one launch (start us, length us, event | category | flops | bytes accessed | tf_op | source)
XLA Modules:
  0.0 145.3 jit_solution(5345054135131809427)
XLA Ops:
  0.6 143.1 %exchange.1 = (bf16[2,128,2048]{2,1,0:T(8,128)(2,1)S(1)}, f32[160,1280]{1,0:T(8,128)S(1)}, f32[160,1280]{1,0:T(8,128)S(1)}) custom-call(s32[2,2,8]{2,1,0:T(2,128)} %bitcast.7, s32[2,2]{1,0:T(2,128)} %links_in.1, s32[2]{0:T(128)} %lengths_in.1, bf16[128,1280]{1,0:T(8,128)(2,1)} %bitcast.5, bf16[128,1280]{1,0:T(8,128)(2,1)} %bitcast.6, f32[1280]{0:T(1024)} %gain_in.1, ...), custom_call_target="tpu_custom_call" | custom-call | tf_op jit(solution)/shard_map/exchange/pallas_call | solution.py:943
  143.7 1.5 %store_outputs.1 = (bf16[2,128,2048]{2,1,0:T(8,128)(2,1)}, f32[160,1280]{1,0:T(8,128)}, f32[160,1280]{1,0:T(8,128)}) custom-call(bf16[2,128,2048]{2,1,0:T(8,128)(2,1)S(1)} %get-tuple-element.6.refs_0_, f32[160,1280]{1,0:T(8,128)S(1)} %get-tuple-element.7.refs_1_, f32[160,1280]{1,0:T(8,128)S(1)} %get-tuple-element.8.refs_2_), custom_call_target="tpu_custom_call" | custom-call | tf_op jit(solution)/shard_map/store_outputs/pallas_call | solution.py:917
